TPU v7x, 32 devices: a 4x2x2 block of a 4x4x8 slice. The times are simulated.
32 devices in a mesh: dp: 4 (over y, z), x: 8 (over x, core).
Axes of the slice: x: 4, y: 2, z: 2, core: 2. Of those that a mesh axis runs over, the one named last changes fastest.
The devices are a block of a 4x4x8 slice.
Arguments:
- start_pos: int32 [512], P('dp'), parts along dimension 0
- hidden_in: bfloat16 [4, 512, 2048], P(None, ('dp', 'x')), parts along dimension 1
- k_cache: bfloat16 [512, 256, 8, 128], P('dp', None, 'x'), parts along dimension 0
- v_cache: bfloat16 [512, 256, 8, 128], P('dp', None, 'x'), parts along dimension 0
- attn_norm: bfloat16 [2048], replicated
- w_q: bfloat16 [2048, 2048], replicated
- w_k: bfloat16 [2048, 1024], replicated
- w_v: bfloat16 [2048, 1024], replicated
- q_norm: bfloat16 [128], replicated
- k_norm: bfloat16 [128], replicated
- w_o: bfloat16 [2048, 2048], replicated
- mlp_norm: bfloat16 [2048], replicated
- w_gate: bfloat16 [2048, 6144], replicated
- w_up: bfloat16 [2048, 6144], replicated
- w_down: bfloat16 [6144, 2048], replicated
Outputs:
- output 1: bfloat16 [4, 512, 2048], P(None, ('dp', 'x')), parts along dimension 1
- output 2: bfloat16 [512, 256, 8, 128], P(('dp', 'x')), parts along dimension 0
- output 3: bfloat16 [512, 256, 8, 128], P(('dp', 'x')), parts along dimension 0
There are 4 independent parts. A program takes and returns all parts, laid end to end along the dimension named above; an argument that names none is the same for every part.
All inputs are finite; a program needn't handle non-finite values.
Results may differ from a plain program's by a relative error of at most 0.010446.
Values are sent between devices in bfloat16 or wider.
A program may use at most 768 MiB of HBM per device.

v0:
```python
import jax
import jax.numpy as jnp
from jax import lax
from jax.sharding import PartitionSpec as P

EPS = 1e-6
THETA = 1000000.0


def rms_norm(values, gain_vec):
    values32 = values.astype(jnp.float32)
    inv_rms = lax.rsqrt(jnp.mean(values32 * values32, axis=-1, keepdims=True) + EPS)
    return values32 * inv_rms * gain_vec.astype(jnp.float32)


def rotary(values, positions):
    head_dim = values.shape[-1]
    half_dim = head_dim // 2
    inv_freq = jnp.power(THETA, -jnp.arange(half_dim, dtype=jnp.float32) * 2.0 / head_dim)
    angles = positions.astype(jnp.float32)[..., None, None] * inv_freq
    cos_part = jnp.cos(angles)
    sin_part = jnp.sin(angles)
    first_half = values[..., :half_dim]
    second_half = values[..., half_dim:]
    return jnp.concatenate([first_half * cos_part - second_half * sin_part, second_half * cos_part + first_half * sin_part], axis=-1)


def project(hidden, positions, attn_norm, w_q, w_k, w_v, q_norm, k_norm):
    n_steps, num_rows = hidden.shape[0], hidden.shape[1]
    head_dim = q_norm.shape[0]
    normed = rms_norm(hidden, attn_norm).astype(jnp.bfloat16)
    queries = jnp.einsum('sbd,de->sbe', normed, w_q, preferred_element_type=jnp.float32).reshape(n_steps, num_rows, -1, head_dim)
    keys_new = jnp.einsum('sbd,de->sbe', normed, w_k, preferred_element_type=jnp.float32).reshape(n_steps, num_rows, -1, head_dim)
    values_new = jnp.einsum('sbd,de->sbe', normed, w_v, preferred_element_type=jnp.float32).reshape(n_steps, num_rows, -1, head_dim)
    queries = rotary(rms_norm(queries, q_norm), positions).astype(jnp.bfloat16)
    keys_new = rotary(rms_norm(keys_new, k_norm), positions).astype(jnp.bfloat16)
    return queries, keys_new, values_new.astype(jnp.bfloat16)


def attend(queries, cache_k, cache_v, keys_new, values_new, start_pos):
    n_steps, num_rows, n_heads, head_dim = queries.shape
    num_slots, kv_local = cache_k.shape[1], cache_k.shape[2]
    grouped = queries.reshape(n_steps, num_rows, kv_local, n_heads // kv_local, head_dim)
    score_scale = head_dim ** -0.5
    old_scores = jnp.einsum('sbkgd,btkd->bkgst', grouped, cache_k, preferred_element_type=jnp.float32) * score_scale
    old_valid = (jnp.arange(num_slots)[None, :] < start_pos[:, None])[:, None, None, None, :]
    old_scores = jnp.where(old_valid, old_scores, -jnp.inf)
    new_scores = jnp.einsum('sbkgd,jbkd->bkgsj', grouped, keys_new, preferred_element_type=jnp.float32) * score_scale
    new_valid = jnp.arange(n_steps)[:, None] >= jnp.arange(n_steps)[None, :]
    new_scores = jnp.where(new_valid, new_scores, -jnp.inf)
    peak_score = jnp.maximum(jnp.max(old_scores, axis=-1, keepdims=True), jnp.max(new_scores, axis=-1, keepdims=True))
    old_weights = jnp.exp(old_scores - peak_score)
    new_weights = jnp.exp(new_scores - peak_score)
    weight_sum = jnp.sum(old_weights, axis=-1) + jnp.sum(new_weights, axis=-1)
    mixed_vals = jnp.einsum('bkgst,btkd->sbkgd', old_weights.astype(jnp.bfloat16), cache_v, preferred_element_type=jnp.float32)
    mixed_vals = mixed_vals + jnp.einsum('bkgsj,jbkd->sbkgd', new_weights.astype(jnp.bfloat16), values_new, preferred_element_type=jnp.float32)
    mixed_vals = mixed_vals / jnp.transpose(weight_sum, (3, 0, 1, 2))[..., None]
    return mixed_vals.astype(jnp.bfloat16).reshape(n_steps, num_rows, n_heads, head_dim)


def finish(hidden, attended, w_o, mlp_norm, w_gate, w_up, w_down):
    n_steps, num_rows = attended.shape[0], attended.shape[1]
    flat_attn = attended.reshape(n_steps, num_rows, -1)
    attn_out = jnp.einsum('sbe,ed->sbd', flat_attn, w_o, preferred_element_type=jnp.float32)
    residual = (hidden.astype(jnp.float32) + attn_out).astype(jnp.bfloat16)
    normed = rms_norm(residual, mlp_norm).astype(jnp.bfloat16)
    gate_val = jnp.einsum('sbd,df->sbf', normed, w_gate, preferred_element_type=jnp.float32)
    up_val = jnp.einsum('sbd,df->sbf', normed, w_up, preferred_element_type=jnp.float32)
    activated = (jax.nn.silu(gate_val) * up_val).astype(jnp.bfloat16)
    down_val = jnp.einsum('sbf,fd->sbd', activated, w_down, preferred_element_type=jnp.float32)
    return (residual.astype(jnp.float32) + down_val).astype(jnp.bfloat16)


def write_slots(cache_arr, fresh_rows, start_pos):
    slot_ids = jnp.arange(cache_arr.shape[1])[None, :, None, None]
    for step_idx in range(fresh_rows.shape[0]):
        slot_hit = slot_ids == (start_pos + step_idx)[:, None, None, None]
        cache_arr = jnp.where(slot_hit, fresh_rows[step_idx][:, None], cache_arr)
    return cache_arr


def solution(mesh):
    row_spec = P(None, ('dp', 'x'), None)
    cache_in = P('dp', None, 'x', None)
    cache_out = P(('dp', 'x'), None, None, None)

    def local_run(start_pos, hidden_in, k_heads, v_heads, attn_norm, w_q, w_k, w_v, q_norm, k_norm, w_o, mlp_norm, w_gate, w_up, w_down):
        num_rows = hidden_in.shape[1]
        my_pos = lax.dynamic_slice_in_dim(start_pos, lax.axis_index('x') * num_rows, num_rows)
        k_local = lax.all_to_all(k_heads, 'x', 0, 2, tiled=True)
        v_local = lax.all_to_all(v_heads, 'x', 0, 2, tiled=True)
        positions = my_pos[None, :] + jnp.arange(hidden_in.shape[0])[:, None]
        queries, keys_new, values_new = project(hidden_in, positions, attn_norm, w_q, w_k, w_v, q_norm, k_norm)
        attended = attend(queries, k_local, v_local, keys_new, values_new, my_pos)
        out_hidden = finish(hidden_in, attended, w_o, mlp_norm, w_gate, w_up, w_down)
        return out_hidden, write_slots(k_local, keys_new, my_pos), write_slots(v_local, values_new, my_pos)

    return jax.shard_map(local_run, mesh=mesh, in_specs=(P('dp'), row_spec, cache_in, cache_in) + (P(),) * 11, out_specs=(row_spec, cache_out, cache_out), check_vma=False)
```

profile of v0, /device:TPU:81, one launch (start us, length us, event | category | flops | bytes accessed | tf_op | source)
XLA Modules:
  0.0 299.3 jit_solution(14174656724736906085)
XLA Ops:
  0.6 101.2 %all_to_all.36 = bf16[128,256,1,128]{3,1,2,0:T(8,128)(2,1)} all-to-all(bf16[128,256,1,128]{3,1,2,0:T(8,128)(2,1)} %param.17), channel_id=1, replica_groups=mesh['dp'=4,'x'=8] {'x'}, dimensions={0} | all-to-all | bytes 16777216 | tf_op jit(solution)/shard_map/all_to_all | solution.py:90
  101.8 6.1 %all-to-all-start.1 = ((bf16[128,256,1,128]{3,1,2,0:T(8,128)(2,1)}), bf16[128,256,1,128]{3,1,2,0:T(8,128)(2,1)}, u32[]{:S(2)}, u32[]{:S(2)}) async-start(bf16[128,256,1,128]{3,1,2,0:T(8,128)(2,1)} %param.18), calls=%async_computation.1 | async-start | bytes 16777216 | tf_op jit(solution)/shard_map/all_to_all | solution.py:91
  108.1 5.0 %fusion.18 = f32[4,16,2048]{2,1,0:T(8,128)S(1)} fusion(bf16[2048,2048]{1,0:T(8,128)(2,1)} %param.20, bf16[4,16,2048]{2,1,0:T(8,128)(2,1)S(1)} %copy-done, f32[2048]{0:T(1024)S(1)} %convert_element_type.62, f32[4,16]{1,0:T(4,128)S(1)} %add_rsqrt_fusion.3), kind=kOutput, calls=%fused_computation.20 | convolution fusion | flops 537395200 | bytes 9183488 | tf_op jit(solution)/shard_map/sbd,de->sbe/dot_general | solution.py:32
  113.4 0.3 multiply_cosine_fusion
  114.2 0.2 subtract_convert_fusion
  114.9 3.1 %fusion.30 = f32[4,16,1024]{2,1,0:T(8,128)S(1)} fusion(bf16[2048,1024]{1,0:T(8,128)(2,1)} %param.21, bf16[4,16,2048]{2,1,0:T(8,128)(2,1)S(1)} %copy-done, f32[2048]{0:T(1024)S(1)} %convert_element_type.62, f32[4,16]{1,0:T(4,128)S(1)} %add_rsqrt_fusion.3), kind=kOutput, calls=%fused_computation.28 | convolution fusion | flops 268959744 | bytes 4727040 | tf_op jit(solution)/shard_map/sbd,de->sbe/dot_general | solution.py:33
  118.4 0.2 fusion.86
  118.9 2.5 fusion.93
  121.4 0.6 copy.95
  122.3 3.1 %fusion.67 = bf16[4,16,1024]{2,1,0:T(8,128)(2,1)S(1)} fusion(bf16[2048,1024]{1,0:T(8,128)(2,1)} %param.22, bf16[4,16,2048]{2,1,0:T(8,128)(2,1)S(1)} %copy-done, f32[2048]{0:T(1024)S(1)} %convert_element_type.62, f32[4,16]{1,0:T(4,128)S(1)} %add_rsqrt_fusion.3), kind=kOutput, calls=%fused_computation.46 | convolution fusion | flops 269025280 | bytes 4595968 | tf_op jit(solution)/shard_map/sbd,de->sbe/dot_general | solution.py:34
  125.5 0.6 slice_maximum_fusion.3
  126.4 5.9 %fusion.105 = (f32[16,8,2,4]{3,2,1,0:T(2,128)S(1)}, f32[16,8,2,4,256]{4,3,2,1,0:T(4,128)S(1)}) fusion(bf16[8,16,256,1,128]{4,2,1,0,3:T(8,128)(2,1)} %bitcast.170, bf16[4,16,8,2,64]{4,0,3,2,1:T(4,128)(2,1)S(1)} %bitcast.179, bf16[4,16,8,2,64]{4,0,3,2,1:T(4,128)(2,1)S(1)} %bitcast.181, pred[16,256]{1,0:T(8,128)(4,1)S(1)} %get-tuple-element.44), kind=kOutput, calls=%fused_computation.120 | convolution fusion | flops 68418560 | bytes 9707520 | tf_op jit(solution)/shard_map/sbkgd,btkd->bkgst/dot_general | solution.py:45
  132.5 0.8 fusion.76
  133.4 68.2 %all-to-all-done.1 = bf16[128,256,1,128]{3,1,2,0:T(8,128)(2,1)} async-done(((bf16[128,256,1,128]{3,1,2,0:T(8,128)(2,1)}), bf16[128,256,1,128]{3,1,2,0:T(8,128)(2,1)}, u32[]{:S(2)}, u32[]{:S(2)}) %all-to-all-start.1) | async-done | bytes 8388640 | tf_op jit(solution)/shard_map/all_to_all | solution.py:91
  201.5 4.8 %fusion.61 = f32[4,16,8,2,128]{4,0,3,2,1:T(4,128)S(1)} fusion(bf16[8,16,256,1,128]{4,2,1,0,3:T(8,128)(2,1)} %bitcast.13, f32[16,8,2,4,256]{4,3,2,1,0:T(4,128)S(1)} %get-tuple-element.46, f32[16,8,2,4]{3,2,1,0:T(2,128)S(1)} %max.8), kind=kOutput, calls=%fused_computation.41 | convolution fusion | flops 67633152 | bytes 9965568 | tf_op jit(solution)/shard_map/bkgst,btkd->sbkgd/dot_general | solution.py:55
  206.5 0.6 copy.100
  207.3 10.6 %add_bitcast_fusion = f32[4,16,8,2]{0,3,2,1:T(2,128)S(1)} fusion(f32[16,8,2,4]{3,2,1,0:T(2,128)S(1)} %fusion.76, f32[16,8,2,4]{3,2,1,0:T(2,128)S(1)} %copy.101), kind=kLoop, calls=%fused_computation.82 | loop fusion | flops 1024 | bytes 12288 | tf_op jit(solution)/shard_map/add | solution.py:54
  217.9 0.4 fusion.66
  218.7 5.0 %multiply_reduce_fusion = (f32[4,16]{1,0:T(4,128)S(1)}, f32[4,16,2048]{2,1,0:T(8,128)S(1)}) fusion(bf16[4,16,2048]{2,1,0:T(8,128)(2,1)S(1)} %reshape_reshape.3, bf16[2048,2048]{1,0:T(8,128)(2,1)} %param.25, bf16[4,16,2048]{2,1,0:T(8,128)(2,1)S(1)} %copy-done), kind=kOutput, calls=%fused_computation.63 | convolution fusion | flops 537657280 | bytes 9437440 | tf_op jit(solution)/shard_map/sbe,ed->sbd/dot_general | solution.py:64
  223.8 16.0 %fusion.12 = (bf16[16,256,8,128]{3,1,2,0:T(8,128)(2,1)}, bf16[16,256,8,128]{3,1,2,0:T(8,128)(2,1)}) fusion(pred[16,256]{1,0:T(8,128)(4,1)S(1)} %get-tuple-element.43, pred[16,256]{1,0:T(8,128)(4,1)S(1)} %get-tuple-element.50, pred[16,256]{1,0:T(8,128)(4,1)S(1)} %get-tuple-element.51, pred[16,256]{1,0:T(8,128)(4,1)S(1)} %get-tuple-element.49, ...), kind=kLoop, calls=%fused_computation.13 | loop fusion | flops 33554432 | bytes 33832960 | tf_op jit(solution)/shard_map/jit(_where)/select_n | solution.py:78
  239.8 13.9 %copy.103 = bf16[16,256,8,128]{3,2,1,0:T(8,128)(2,1)} copy(bf16[16,256,8,128]{3,1,2,0:T(8,128)(2,1)} %get-tuple-element.38) | data formatting | bytes 16777216
  253.6 14.0 %copy.104 = bf16[16,256,8,128]{3,2,1,0:T(8,128)(2,1)} copy(bf16[16,256,8,128]{3,1,2,0:T(8,128)(2,1)} %get-tuple-element.37) | data formatting | bytes 16777216
  267.7 10.5 %fusion.4 = f32[4,16,6144]{2,1,0:T(8,128)S(1)} fusion(bf16[2048,6144]{1,0:T(8,128)(2,1)} %param.27, f32[4,16,2048]{2,1,0:T(8,128)S(1)} %get-tuple-element.48, f32[2048]{0:T(1024)S(1)} %convert_element_type.74, f32[4,16]{1,0:T(4,128)S(1)} %add_rsqrt_fusion.2), kind=kOutput, calls=%fused_computation.4 | convolution fusion | flops 1611005952 | bytes 27271424 | tf_op jit(solution)/shard_map/sbd,df->sbf/dot_general | solution.py:67
  278.2 20.7 %fusion.48 = bf16[4,16,2048]{2,1,0:T(8,128)(2,1)} fusion(f32[4,16,2048]{2,1,0:T(8,128)S(1)} %get-tuple-element.48, bf16[6144,2048]{1,0:T(8,128)(2,1)} %param.29, bf16[2048,6144]{1,0:T(8,128)(2,1)} %param.28, f32[4,16,6144]{2,1,0:T(8,128)S(1)} %fusion.4, f32[2048]{0:T(1024)S(1)} %convert_element_type.74, f32[4,16]{1,0:T(4,128)S(1)} %add_rsqrt_fusion.2), kind=kOutput, calls=%fused_computation.34 | convolution fusion | flops 3224240128 | bytes 52699392 | tf_op jit(solution)/shard_map/sbf,fd->sbd/dot_general | solution.py:70
  (57 shorter events, 3.4 us)
Async XLA Ops:
  101.8 6.1 %copy-start.4 = (bf16[128]{0:T(256)(128)(2,1)S(1)}, bf16[128]{0:T(256)(128)(2,1)}, u32[]{:S(2)}) copy-start(bf16[128]{0:T(256)(128)(2,1)} %param.23) | copy-start | bytes 772
  101.8 6.1 %copy-start.1 = (bf16[2048]{0:T(1024)(128)(2,1)S(1)}, bf16[2048]{0:T(1024)(128)(2,1)}, u32[]{:S(2)}) copy-start(bf16[2048]{0:T(1024)(128)(2,1)} %param.19) | copy-start | bytes 12292
  101.8 6.1 %copy-start = (bf16[4,16,2048]{2,1,0:T(8,128)(2,1)S(1)}, bf16[4,16,2048]{2,1,0:T(8,128)(2,1)}, u32[]{:S(2)}) copy-start(bf16[4,16,2048]{2,1,0:T(8,128)(2,1)} %param.16) | copy-start | bytes 786436
  101.8 99.7 %all-to-all-start.1 = ((bf16[128,256,1,128]{3,1,2,0:T(8,128)(2,1)}), bf16[128,256,1,128]{3,1,2,0:T(8,128)(2,1)}, u32[]{:S(2)}, u32[]{:S(2)}) async-start(bf16[128,256,1,128]{3,1,2,0:T(8,128)(2,1)} %param.18), calls=%async_computation.1 | async-start | bytes 16777216 | tf_op jit(solution)/shard_map/all_to_all | solution.py:91
  107.9 5.3 %copy-start.3 = (s32[128]{0:T(128)S(1)}, s32[128]{0:T(128)}, u32[]{:S(2)}) copy-start(s32[128]{0:T(128)} %param.15) | copy-start | bytes 1540
  113.1 4.9 %copy-start.5 = (bf16[128]{0:T(256)(128)(2,1)S(1)}, bf16[128]{0:T(256)(128)(2,1)}, u32[]{:S(2)}) copy-start(bf16[128]{0:T(256)(128)(2,1)} %param.24) | copy-start | bytes 772
  114.9 10.6 %copy-start.2 = (bf16[2048]{0:T(1024)(128)(2,1)S(1)}, bf16[2048]{0:T(1024)(128)(2,1)}, u32[]{:S(2)}) copy-start(bf16[2048]{0:T(1024)(128)(2,1)} %param.26) | copy-start | bytes 12292
where the time goes:
time: 304 us; the launch traced here: 299 us
  blocking collectives  101 us (33%)
  waiting for transfers between devices  68.2 us (22%)
  matrix products  61 us (20%)
  local copies, waits for them, and re-layouts  31 us (10%)
  other arithmetic  30.4 us (10%)
  starting transfers between devices  6.11 us (2%)
    all_to_all x1, blocking collectives, local_run(): k_local = lax.all_to_all(k_heads, 'x', 0, 2, tiled=True)  101 us
    all_to_all x1, waiting for transfers between devices, local_run(): v_local = lax.all_to_all(v_heads, 'x', 0, 2, tiled=True)  68.2 us
    unnamed x24, local copies, waits for them, and re-layouts  28.1 us
    dot_general x1, matrix products, finish(): jnp.einsum('sbf,fd->sbd', activated, w_down, preferred_element_type=jnp.f...  20.7 us
    select_n x1, other arithmetic, write_slots(): cache_arr = jnp.where(slot_hit, fresh_rows[step_idx][:, None], cache_arr)  16 us
    add x1, other arithmetic, attend(): weight_sum = jnp.sum(old_weights, axis=-1) + jnp.sum(new_weights, axis=-1)  10.6 us
    dot_general x1, matrix products, finish(): jnp.einsum('sbd,df->sbf', normed, w_gate, preferred_element_type=jnp.floa...  10.5 us
    all_to_all x1, starting transfers between devices, local_run(): v_local = lax.all_to_all(v_heads, 'x', 0, 2, tiled=True)  6.11 us
  transfers between devices with their start and end apart: 1, of which 1 were waited for; matrix products, arithmetic and copies ran while one was open for 8% of the time, Pallas kernels for 0%

commit v1 on v0

v1 whole, which is shorter than its diff:
```python
import functools

import jax
import jax.numpy as jnp
import numpy as np
from jax import lax
from jax.experimental import pallas as pl
from jax.experimental.pallas import tpu as pltpu
from jax.sharding import PartitionSpec as P

EPS = 1e-6
THETA = 1000000.0
F32 = jnp.float32
BF16 = jnp.bfloat16
MESH = pl.DeviceIdType.MESH
TILE = 512
SETS = (1, 1)


def rms(values, gain):
    inv_rms = lax.rsqrt(jnp.mean(values * values, axis=-1, keepdims=True) + EPS)
    return values * inv_rms * gain


def layer_kernel(
    n, steps, rows, heads, hd,
    pos_ref, freq_ref, hid_ref, k_hbm, v_hbm, an_ref, wq_hbm, wk_hbm, wv_hbm, qn_ref, kn_ref, wo_hbm, mn_ref,
    wg_hbm, wu_hbm, wd_hbm,
    out_ref, knew_ref, vnew_ref, rk_hbm, rv_hbm,
    hid_s, act_s, x1_s, acc_s, tmp_s, cs_s, sn_s, msg_s, msg_r, o_s, o_r, kbuf, vbuf, wbuf, ubuf, dbuf,
    wsem, usem, dsem, ksem, vsem, own_sem, msg_ss, msg_rs, o_ss, o_rs, bulk_s, bulk_r,
):
    me = lax.axis_index("x")
    num = steps * rows
    q_per = heads // n
    q_rows = q_per * num
    barrier = pltpu.get_barrier_semaphore()

    def peer(o):
        return lax.rem(me + o, n)

    for o in range(1, n):
        pl.semaphore_signal(barrier, inc=1, device_id={"x": peer(o)}, device_id_type=MESH)
    pl.semaphore_wait(barrier, n - 1)

    part = rows // 4
    rounds = 2 * (rows // part)
    order = (2, 6, 4, 3, 7, 5, 1) if n == 8 else tuple(range(1, n))

    def send_round(src, dst, which, first):
        for o in order:
            to = peer(o)
            pltpu.make_async_remote_copy(
                src_ref=src.at[pl.ds(to * rows + first, part)],
                dst_ref=dst.at[me, pl.ds(first, part)],
                send_sem=bulk_s.at[which], recv_sem=bulk_r.at[which], device_id={"x": to}, device_id_type=MESH,
            ).start()

    def bulk(lo, hi):
        def go(src, dst, which, a, b):
            if b > a:
                @pl.loop(a, b)
                def _(r):
                    send_round(src, dst, which, r * part)
        half = rounds // 2
        go(k_hbm, rk_hbm, 0, min(lo, half), min(hi, half))
        go(v_hbm, rv_hbm, 1, max(lo, half) - half, max(hi, half) - half)

    bulk(0, SETS[0])

    def cols(hbm, i):
        return hbm.at[:, pl.ds(pl.multiple_of(i * TILE, TILE), TILE)]

    def load(src, dst, sem, slot):
        return pltpu.make_async_copy(src, dst.at[slot], sem.at[slot])

    def stream(hbm, body):
        tiles = hbm.shape[1] // TILE
        load(cols(hbm, 0), wbuf, wsem, 0).start()

        @pl.loop(0, tiles)
        def _(i):
            slot = lax.rem(i, 2)

            @pl.when(i + 1 < tiles)
            def _():
                load(cols(hbm, i + 1), wbuf, wsem, 1 - slot).start()

            load(cols(hbm, i), wbuf, wsem, slot).wait()
            body(i, wbuf[slot])

    dim = hid_ref.shape[2]
    for c in range(0, dim, hd):
        for s in range(steps):
            tmp_s[pl.ds(s, rows, stride=steps), :] = hid_ref[s, :, c : c + hd].astype(F32)
        hid_s[:, c : c + hd] = tmp_s[...]
    act_s[...] = rms(hid_s[...], an_ref[...].astype(F32)).astype(BF16)

    row = lax.broadcasted_iota(jnp.int32, (num, hd), 0)
    pos = jnp.zeros((num, hd), jnp.int32)
    for b in range(rows):
        pos = jnp.where(row // steps == b, pos_ref[me * rows + b], pos)
    angles = (pos + row % steps).astype(F32) * freq_ref[...]
    lane = lax.broadcasted_iota(jnp.int32, (num, hd), 1)
    cs_s[...] = jnp.cos(angles)
    sn_s[...] = jnp.where(lane < hd // 2, -jnp.sin(angles), jnp.sin(angles))

    def rotate(v):
        return v * cs_s[...] + pltpu.roll(v, hd // 2, 1) * sn_s[...]

    per_tile = TILE // hd

    def q_tile(i, w):
        y = jnp.dot(act_s[...], w, preferred_element_type=F32)
        gain = qn_ref[...].astype(F32)
        for g in range(per_tile // q_per):
            pair = []
            for j in range(q_per):
                c = (g * q_per + j) * hd
                head = rotate(rms(y[:, c : c + hd], gain))
                pair.append(head.reshape(num // 8, 8, hd))
            both = jnp.concatenate(pair, axis=1).reshape(q_rows, hd)
            msg_s[i * (per_tile // q_per) + g, 0:q_rows, :] = both.astype(BF16)

    def k_tile(i, w):
        y = jnp.dot(act_s[...], w, preferred_element_type=F32)
        gain = kn_ref[...].astype(F32)
        for g in range(per_tile):
            head = rotate(rms(y[:, g * hd : (g + 1) * hd], gain)).astype(BF16)
            msg_s[i * per_tile + g, q_rows : q_rows + num, :] = head

    def v_tile(i, w):
        y = jnp.dot(act_s[...], w, preferred_element_type=F32).astype(BF16)
        for g in range(per_tile):
            msg_s[i * per_tile + g, q_rows + num : q_rows + 2 * num, :] = y[:, g * hd : (g + 1) * hd]

    stream(wq_hbm, q_tile)
    stream(wk_hbm, k_tile)
    stream(wv_hbm, v_tile)

    def msg_copy(to):
        return pltpu.make_async_remote_copy(
            src_ref=msg_s.at[to], dst_ref=msg_r.at[me], send_sem=msg_ss.at[to], recv_sem=msg_rs.at[me],
            device_id={"x": to}, device_id_type=MESH,
        )

    def msg_arrival(source):
        return pltpu.make_async_remote_copy(
            src_ref=msg_s.at[source], dst_ref=msg_r.at[source], send_sem=msg_ss.at[source], recv_sem=msg_rs.at[source],
            device_id={"x": source}, device_id_type=MESH,
        )

    def o_copy(to):
        return pltpu.make_async_remote_copy(
            src_ref=o_s.at[to], dst_ref=o_r.at[me], send_sem=o_ss.at[to], recv_sem=o_rs.at[me],
            device_id={"x": to}, device_id_type=MESH,
        )

    def o_arrival(source):
        return pltpu.make_async_remote_copy(
            src_ref=o_s.at[source], dst_ref=o_r.at[source], send_sem=o_ss.at[source], recv_sem=o_rs.at[source],
            device_id={"x": source}, device_id_type=MESH,
        )

    def kv_load(o, slot):
        first = peer(o) * rows
        return (
            pltpu.make_async_copy(k_hbm.at[pl.ds(first, rows)], kbuf.at[slot], ksem.at[slot]),
            pltpu.make_async_copy(v_hbm.at[pl.ds(first, rows)], vbuf.at[slot], vsem.at[slot]),
        )

    for c in kv_load(0, 0):
        c.start()
    for o in range(1, n):
        msg_copy(peer(o)).start()
    bulk(SETS[0], SETS[0] + SETS[1])
    msg_r[me] = msg_s[me]
    for h in range(n):
        knew_ref[:, h * hd : (h + 1) * hd] = msg_s[h, q_rows : q_rows + num, :]
        vnew_ref[:, h * hd : (h + 1) * hd] = msg_s[h, q_rows + num : q_rows + 2 * num, :]

    slots = k_hbm.shape[1]
    scale = hd ** -0.5
    tall = 8 * q_per
    nt = (((1,), (1,)), ((), ()))
    own = [
        pltpu.make_async_copy(kbuf.at[0], rk_hbm.at[me], own_sem.at[0]),
        pltpu.make_async_copy(vbuf.at[0], rv_hbm.at[me], own_sem.at[1]),
    ]

    @pl.loop(0, n)
    def _(o):
        slot = lax.rem(o, 2)
        source = peer(o)

        @pl.when(o == 1)
        def _():
            for c in own:
                c.wait()

        @pl.when(o + 1 < n)
        def _():
            for c in kv_load(o + 1, 1 - slot):
                c.start()

        for c in kv_load(o, slot):
            c.wait()

        @pl.when(o == 0)
        def _():
            for c in own:
                c.start()

        @pl.when(o > 0)
        def _():
            msg_arrival(source).wait_recv()

        k_new = msg_r[source, q_rows : q_rows + num, :]
        v_new = msg_r[source, q_rows + num : q_rows + 2 * num, :]
        fresh = lax.dot_general(msg_r[source, 0:q_rows, :], k_new, nt, preferred_element_type=F32) * scale
        r = lax.broadcasted_iota(jnp.int32, (q_rows, num), 0)
        c = lax.broadcasted_iota(jnp.int32, (q_rows, num), 1)
        seq = (r // tall) * (8 // steps) + (r % 8) // steps
        fresh = jnp.where((c // steps == seq) & (c % steps <= r % steps), fresh, -jnp.inf)
        in_pair = (lax.broadcasted_iota(jnp.int32, (tall, slots), 0) % 8) // steps
        in_pair_o = (lax.broadcasted_iota(jnp.int32, (tall, hd), 0) % 8) // steps
        t = lax.broadcasted_iota(jnp.int32, (tall, slots), 1)
        for i in range(q_rows // tall):
            q = msg_r[source, i * tall : (i + 1) * tall, :]
            b = i * (8 // steps)
            old = lax.dot_general(q, kbuf[slot, b], nt, preferred_element_type=F32)
            start = jnp.full((tall, slots), pos_ref[source * rows + b], jnp.int32)
            for e in range(1, 8 // steps):
                other = lax.dot_general(q, kbuf[slot, b + e], nt, preferred_element_type=F32)
                old = jnp.where(in_pair == e, other, old)
                start = jnp.where(in_pair == e, pos_ref[source * rows + b + e], start)
            old = jnp.where(t < start, old * scale, -jnp.inf)
            new = fresh[i * tall : (i + 1) * tall, :]
            peak = jnp.maximum(jnp.max(old, axis=-1, keepdims=True), jnp.max(new, axis=-1, keepdims=True))
            old = jnp.exp(old - peak)
            new = jnp.exp(new - peak)
            total = jnp.sum(old, axis=-1, keepdims=True) + jnp.sum(new, axis=-1, keepdims=True)
            weights = old.astype(BF16)
            mixed = jnp.dot(weights, vbuf[slot, b], preferred_element_type=F32)
            for e in range(1, 8 // steps):
                other = jnp.dot(weights, vbuf[slot, b + e], preferred_element_type=F32)
                mixed = jnp.where(in_pair_o == e, other, mixed)
            mixed = mixed + jnp.dot(new.astype(BF16), v_new, preferred_element_type=F32)
            o_s[source, i * tall : (i + 1) * tall, :] = (mixed / total).astype(BF16)

        @pl.when(o == 0)
        def _():
            o_r[me] = o_s[me]

        @pl.when(o > 0)
        def _():
            o_copy(source).start()

    bulk(SETS[0] + SETS[1], rounds)

    for o in range(1, n):
        o_arrival(peer(o)).wait_recv()
    for h in range(n):
        both = o_r[h].astype(F32).reshape(num // 8, tall, hd)
        for j in range(q_per):
            head = both[:, j * 8 : (j + 1) * 8, :].reshape(num, hd)
            act_s[:, (h * q_per + j) * hd : (h * q_per + j + 1) * hd] = head.astype(BF16)

    def wo_tile(i, w):
        at = pl.ds(pl.multiple_of(i * TILE, TILE), TILE)
        y = jnp.dot(act_s[...], w, preferred_element_type=F32)
        x1_s[:, at] = (hid_s[:, at] + y).astype(BF16).astype(F32)

    stream(wo_hbm, wo_tile)
    act_s[...] = rms(x1_s[...], mn_ref[...].astype(F32)).astype(BF16)
    acc_s[...] = jnp.zeros_like(acc_s)
    tiles = wg_hbm.shape[1] // TILE

    def mlp_loads(i, slot):
        at = pl.ds(pl.multiple_of(i * TILE, TILE), TILE)
        return (
            load(cols(wg_hbm, i), wbuf, wsem, slot),
            load(cols(wu_hbm, i), ubuf, usem, slot),
            load(wd_hbm.at[at, :], dbuf, dsem, slot),
        )

    for c in mlp_loads(0, 0):
        c.start()

    @pl.loop(0, tiles)
    def _(i):
        slot = lax.rem(i, 2)

        @pl.when(i + 1 < tiles)
        def _():
            for c in mlp_loads(i + 1, 1 - slot):
                c.start()

        for c in mlp_loads(i, slot):
            c.wait()
        z = act_s[...]
        gate = jnp.dot(z, wbuf[slot], preferred_element_type=F32)
        up = jnp.dot(z, ubuf[slot], preferred_element_type=F32)
        g = (jax.nn.silu(gate) * up).astype(BF16)
        acc_s[...] += jnp.dot(g, dbuf[slot], preferred_element_type=F32)

    for c in range(0, dim, hd):
        tmp_s[...] = x1_s[:, c : c + hd] + acc_s[:, c : c + hd]
        for s in range(steps):
            out_ref[s, :, c : c + hd] = tmp_s[pl.ds(s, rows, stride=steps), :].astype(BF16)

    for o in range(1, n):
        msg_copy(peer(o)).wait_send()
        o_copy(peer(o)).wait_send()
    for which, dst in enumerate((rk_hbm, rv_hbm)):
        whole = dst.at[pl.ds(0, n - 1)]
        pltpu.make_async_copy(whole, whole, bulk_s.at[which]).wait()
        pltpu.make_async_copy(whole, whole, bulk_r.at[which]).wait()


def place_kernel(steps, pos_ref, rk_ref, rv_ref, kn_ref, vn_ref, ko_ref, vo_ref, scr):
    b = pl.program_id(0)
    n, hd = rk_ref.shape[0], rk_ref.shape[-1]
    slots = rk_ref.shape[2]
    for src, new, dst in ((rk_ref, kn_ref, ko_ref), (rv_ref, vn_ref, vo_ref)):
        for h in range(n):
            scr[pl.ds(h, slots, stride=n), :] = src[h, 0].astype(F32)
        dst[0] = scr[...].reshape(slots, n, hd).astype(BF16)
        for s in range(steps):
            dst[0, pos_ref[b] + s] = new[b * steps + s]


def solution(mesh):
    row_spec = P(None, ("dp", "x"), None)
    cache_in = P("dp", None, "x", None)
    cache_out = P(("dp", "x"), None, None, None)
    n = mesh.shape["x"]

    def local_run(start_pos, hidden_in, k_heads, v_heads, attn_norm, w_q, w_k, w_v, q_norm, k_norm, w_o, mlp_norm, w_gate, w_up, w_down):
        steps, rows, dim = hidden_in.shape
        slots, hd = k_heads.shape[1], k_heads.shape[3]
        heads = w_q.shape[1] // hd
        num = steps * rows
        half = hd // 2
        inv_freq = np.power(np.float32(THETA), -np.arange(half, dtype=np.float32) * np.float32(2.0) / np.float32(hd))
        freq = jnp.asarray(np.concatenate([inv_freq, inv_freq])[None, :], F32)
        vmem = pl.BlockSpec(memory_space=pltpu.VMEM)
        hbm = pl.BlockSpec(memory_space=pltpu.HBM)
        smem = pl.BlockSpec(memory_space=pltpu.SMEM)
        q_rows = (heads // n) * num
        dma = pltpu.SemaphoreType.DMA
        blocks = jax.ShapeDtypeStruct((n, rows, slots, hd), BF16)
        fresh = jax.ShapeDtypeStruct((num, n * hd), BF16)
        out, k_new, v_new, rk, rv = pl.pallas_call(
            functools.partial(layer_kernel, n, steps, rows, heads, hd),
            name="layer",
            out_shape=(jax.ShapeDtypeStruct(hidden_in.shape, BF16), fresh, fresh, blocks, blocks),
            in_specs=[smem, vmem, vmem, hbm, hbm, vmem, hbm, hbm, hbm, vmem, vmem, hbm, vmem, hbm, hbm, hbm],
            out_specs=(vmem, vmem, vmem, hbm, hbm),
            scratch_shapes=[
                pltpu.VMEM((num, dim), F32), pltpu.VMEM((num, dim), BF16), pltpu.VMEM((num, dim), F32), pltpu.VMEM((num, dim), F32),
                pltpu.VMEM((num, hd), F32), pltpu.VMEM((num, hd), F32), pltpu.VMEM((num, hd), F32),
                pltpu.VMEM((n, q_rows + 2 * num, hd), BF16), pltpu.VMEM((n, q_rows + 2 * num, hd), BF16),
                pltpu.VMEM((n, q_rows, hd), BF16), pltpu.VMEM((n, q_rows, hd), BF16),
                pltpu.VMEM((2, rows, slots, hd), BF16), pltpu.VMEM((2, rows, slots, hd), BF16),
                pltpu.VMEM((2, dim, TILE), BF16), pltpu.VMEM((2, dim, TILE), BF16), pltpu.VMEM((2, TILE, dim), BF16),
                dma((2,)), dma((2,)), dma((2,)), dma((2,)), dma((2,)), dma((2,)),
                dma((n,)), dma((n,)), dma((n,)), dma((n,)), dma((2,)), dma((2,)),
            ],
            compiler_params=pltpu.CompilerParams(collective_id=0, has_side_effects=True, vmem_limit_bytes=60 * 2**20),
        )(
            start_pos, freq, hidden_in, k_heads.reshape(-1, slots, hd), v_heads.reshape(-1, slots, hd), attn_norm.reshape(1, -1),
            w_q, w_k, w_v, q_norm.reshape(1, -1), k_norm.reshape(1, -1), w_o, mlp_norm.reshape(1, -1), w_gate, w_up, w_down,
        )
        my_pos = lax.dynamic_slice_in_dim(start_pos, lax.axis_index("x") * rows, rows)
        in_block = pl.BlockSpec((n, 1, slots, hd), lambda b: (0, b, 0, 0))
        out_block = pl.BlockSpec((1, slots, n, hd), lambda b: (b, 0, 0, 0))
        new_block = pl.BlockSpec((num, n, hd), lambda b: (0, 0, 0))
        cache = jax.ShapeDtypeStruct((rows, slots, n, hd), BF16)
        k_out, v_out = pl.pallas_call(
            functools.partial(place_kernel, steps),
            name="place",
            grid=(rows,),
            out_shape=(cache, cache),
            in_specs=[smem, in_block, in_block, new_block, new_block],
            out_specs=(out_block, out_block),
            scratch_shapes=[pltpu.VMEM((slots * n, hd), F32)],
            compiler_params=pltpu.CompilerParams(dimension_semantics=("arbitrary",), vmem_limit_bytes=60 * 2**20),
        )(my_pos, rk, rv, k_new.reshape(num, n, hd), v_new.reshape(num, n, hd))
        return out, k_out, v_out

    return jax.shard_map(local_run, mesh=mesh, in_specs=(P("dp"), row_spec, cache_in, cache_in) + (P(),) * 11, out_specs=(row_spec, cache_out, cache_out), check_vma=False)
```

time: 304 us -> 225 us (0.74); the launches traced: 299 us -> 224 us
  Pallas kernels: 0 us -> 216 us
  blocking collectives: 101 us -> 0 us
  waiting for transfers between devices: 68.2 us -> 0 us
  matrix products: 61 us -> 0 us
  other arithmetic: 30.4 us -> 0 us
  local copies, waits for them, and re-layouts: 31 us -> 7.75 us
  starting transfers between devices: 6.11 us -> 0 us
    pallas_call x0 -> x2, Pallas kernels: none -> 216 us  [the longest x1 197 us: local_run(): pl.pallas_call(functools.partial(layer_kernel, n, steps, rows, heads, hd)...]
    all_to_all x1 -> x0, blocking collectives: 101 us -> none  [local_run(): k_local = lax.all_to_all(k_heads, 'x', 0, 2, tiled=True)]
    all_to_all x1 -> x0, waiting for transfers between devices: 68.2 us -> none  [local_run(): v_local = lax.all_to_all(v_heads, 'x', 0, 2, tiled=True)]
    dot_general x10 -> x0, matrix products: 61 us -> none  [the longest x1 20.7 us: finish(): jnp.einsum('sbf,fd->sbd', activated, w_down, preferred_element_type=jnp.f...]
    unnamed x24 -> x5, local copies, waits for them, and re-layouts: 28.1 us -> 3.86 us
    select_n x1 -> x0, other arithmetic: 16 us -> none  [write_slots(): cache_arr = jnp.where(slot_hit, fresh_rows[step_idx][:, None], cache_arr)]
    add x3 -> x0, other arithmetic: 10.7 us -> none  [the longest x1 10.6 us: attend(): weight_sum = jnp.sum(old_weights, axis=-1) + jnp.sum(new_weights, axis=-1)]
    all_to_all x1 -> x0, starting transfers between devices: 6.11 us -> none  [local_run(): v_local = lax.all_to_all(v_heads, 'x', 0, 2, tiled=True)]
  transfers between devices with their start and end apart: 1 -> 0, of which waited for: 1 -> 0; matrix products, arithmetic and copies ran while one was open for 8% -> 0% of each run, Pallas kernels for 0% -> 0%
where the time goes in v1:
time: 225 us; the launch traced here: 224 us
  Pallas kernels  216 us (96%)
  local copies, waits for them, and re-layouts  7.75 us (3%)
    pallas_call x1, Pallas kernels, local_run(): pl.pallas_call(functools.partial(layer_kernel, n, steps, rows, heads, hd)...  197 us
    pallas_call x1, Pallas kernels, local_run(): pl.pallas_call(functools.partial(place_kernel, steps), name='place', grid...  18.9 us

profile of v1, /device:TPU:81, one launch (start us, length us, event | category | flops | bytes accessed | tf_op | source)
XLA Modules:
  0.0 224.4 jit_solution(15822920700847201327)
XLA Ops:
  0.6 1.3 dynamic_slice.3.pos_ref
  1.9 1.3 reshape.32.an_ref
  3.2 1.3 reshape.35.mn_ref
  4.5 197.1 %layer.1 = (bf16[4,16,2048]{2,1,0:T(8,128)(2,1)}, bf16[64,1024]{1,0:T(8,128)(2,1)}, bf16[64,1024]{1,0:T(8,128)(2,1)}, bf16[8,16,256,128]{3,2,1,0:T(8,128)(2,1)}, bf16[8,16,256,128]{3,2,1,0:T(8,128)(2,1)}) custom-call(s32[128]{0:T(128)} %pos_ref.1, f32[1,128]{1,0:T(1,128)} %constant.12.clone.freq_ref, bf16[4,16,2048]{2,1,0:T(8,128)(2,1)} %hid_ref.1, ...), custom_call_target="tpu_custom_call" | custom-call | tf_op jit(solution)/shard_map/layer/pallas_call | solution.py:354
  201.6 1.6 copy.19
  203.2 1.6 copy.20
  204.8 0.0 copy-start
  204.8 18.9 %place.1 = (bf16[16,256,8,128]{3,2,1,0:T(8,128)(2,1)}, bf16[16,256,8,128]{3,2,1,0:T(8,128)(2,1)}) custom-call(s32[16]{0:T(128)} %dynamic_slice.3.pos_ref, bf16[8,16,256,128]{3,2,1,0:T(8,128)(2,1)} %get-tuple-element.11.rk_ref, bf16[8,16,256,128]{3,2,1,0:T(8,128)(2,1)} %get-tuple-element.12.rv_ref, bf16[64,8,128]{2,1,0:T(8,128)(2,1)} %bitcast.10, ...), custom_call_target="tpu_custom_call" | custom-call | tf_op jit(solution)/shard_map/place/pallas_call | solution.py:380
  223.7 0.0 copy-done
  223.7 0.7 copy.22
Async XLA Ops:
  204.8 18.9 %copy-start = (bf16[4,16,2048]{2,1,0:T(8,128)(2,1)S(1)}, bf16[4,16,2048]{2,1,0:T(8,128)(2,1)}, u32[]{:S(2)}) copy-start(bf16[4,16,2048]{2,1,0:T(8,128)(2,1)} %get-tuple-element.20) | copy-start | bytes 786436

commit v2 on v1

v2 whole, which is shorter than its diff:
```python
import functools

import jax
import jax.numpy as jnp
import numpy as np
from jax import lax
from jax.experimental import pallas as pl
from jax.experimental.pallas import tpu as pltpu
from jax.sharding import PartitionSpec as P

EPS = 1e-6
THETA = 1000000.0
F32 = jnp.float32
BF16 = jnp.bfloat16
MESH = pl.DeviceIdType.MESH
TILE = 512
PAIR = 2
AWAY = 3
VMEM_LIMIT = 44 * 2**20
AHEAD = 4


def rms(values, gain):
    inv_rms = lax.rsqrt(jnp.mean(values * values, axis=-1, keepdims=True) + EPS)
    return values * inv_rms * gain


def layer_kernel(
    n, steps, rows, heads, hd,
    pos_ref, freq_ref, hid_ref, k_hbm, v_hbm, an_ref, wq_hbm, wk_hbm, wv_hbm, qn_ref, kn_ref, wo_hbm, mn_ref,
    wg_hbm, wu_hbm, wd_hbm,
    out_ref, knew_ref, vnew_ref, ka_ref, va_ref,
    hid_s, act_s, x1_s, acc_s, tmp_s, cs_s, sn_s, msg_s, msg_r, o_s, o_r, rk, rv, kbuf, vbuf, wbuf, ubuf, dbuf, mix_s, kmix_s, vmix_s,
    wsem, usem, dsem, ksem, vsem, own_sem, msg_ss, msg_rs, o_ss, o_rs, bulk_s, krs, vrs,
):
    me = lax.axis_index("x")
    num = steps * rows
    q_per = heads // n
    pairs = rows // PAIR
    home = pairs - AWAY
    slots = k_hbm.shape[1]
    dim = hid_ref.shape[2]
    tall = PAIR * steps * q_per
    new = PAIR * steps
    barrier = pltpu.get_barrier_semaphore()

    def peer(o):
        return lax.rem(me + o, n)

    for o in range(1, n):
        pl.semaphore_signal(barrier, inc=1, device_id={"x": peer(o)}, device_id_type=MESH)
    pl.semaphore_wait(barrier, n - 1)

    order = (2, 6, 4, 3, 7, 5, 1) if n == 8 else tuple(range(1, n))

    def bulk(r):
        for which, (src, dst, arrived) in enumerate(((k_hbm, rk, krs), (v_hbm, rv, vrs))):
            for o in order:
                to = peer(o)
                pltpu.make_async_remote_copy(
                    src_ref=src.at[pl.ds(to * rows + r * PAIR, PAIR)],
                    dst_ref=dst.at[me, pl.ds(r * PAIR, PAIR)],
                    send_sem=bulk_s.at[which], recv_sem=arrived.at[r], device_id={"x": to}, device_id_type=MESH,
                ).start()

    def bulk_wait(r):
        for dst, arrived in ((rk, krs), (rv, vrs)):
            whole = dst.at[pl.ds(0, n - 1), pl.ds(0, PAIR)]
            pltpu.make_async_copy(whole, whole, arrived.at[r]).wait()

    for r in range(2):
        bulk(r)

    own = [
        pltpu.make_async_copy(k_hbm.at[pl.ds(me * rows, rows)], rk.at[me], own_sem.at[0]),
        pltpu.make_async_copy(v_hbm.at[pl.ds(me * rows, rows)], rv.at[me], own_sem.at[1]),
    ]

    def cols(hbm, i):
        return hbm.at[:, pl.ds(pl.multiple_of(i * TILE, TILE), TILE)]

    def load(src, dst, sem, slot):
        return pltpu.make_async_copy(src, dst.at[slot], sem.at[slot])

    def stream(hbm, body):
        tiles = hbm.shape[1] // TILE
        load(cols(hbm, 0), wbuf, wsem, 0).start()

        @pl.loop(0, tiles)
        def _(i):
            slot = lax.rem(i, 2)

            @pl.when(i + 1 < tiles)
            def _():
                load(cols(hbm, i + 1), wbuf, wsem, 1 - slot).start()

            load(cols(hbm, i), wbuf, wsem, slot).wait()
            body(i, wbuf[slot])

    for c in range(0, dim, hd):
        for s in range(steps):
            tmp_s[pl.ds(s, rows, stride=steps), :] = hid_ref[s, :, c : c + hd].astype(F32)
        hid_s[:, c : c + hd] = tmp_s[...]
    act_s[...] = rms(hid_s[...], an_ref[...].astype(F32).reshape(1, dim)).astype(BF16)

    row = lax.broadcasted_iota(jnp.int32, (num, hd), 0)
    pos = jnp.zeros((num, hd), jnp.int32)
    for b in range(rows):
        pos = jnp.where(row // steps == b, pos_ref[me * rows + b], pos)
    angles = (pos + row % steps).astype(F32) * freq_ref[...]
    lane = lax.broadcasted_iota(jnp.int32, (num, hd), 1)
    cs_s[...] = jnp.cos(angles)
    sn_s[...] = jnp.where(lane < hd // 2, -jnp.sin(angles), jnp.sin(angles))

    def rotate(v):
        return v * cs_s[...] + pltpu.roll(v, hd // 2, 1) * sn_s[...]

    per_tile = TILE // hd

    def q_tile(i, w):
        y = jnp.dot(act_s[...], w, preferred_element_type=F32)
        gain = qn_ref[...].astype(F32)
        for g in range(per_tile // q_per):
            parts = []
            for j in range(q_per):
                c = (g * q_per + j) * hd
                head = rotate(rms(y[:, c : c + hd], gain))
                parts.append(head.reshape(pairs, new, hd))
            msg_s[i * (per_tile // q_per) + g, :, 0:tall, :] = jnp.concatenate(parts, axis=1).astype(BF16)

    def k_tile(i, w):
        y = jnp.dot(act_s[...], w, preferred_element_type=F32)
        gain = kn_ref[...].astype(F32)
        for g in range(per_tile):
            head = rotate(rms(y[:, g * hd : (g + 1) * hd], gain))
            msg_s[i * per_tile + g, :, tall : tall + new, :] = head.reshape(pairs, new, hd).astype(BF16)
            kmix_s[pl.ds(i * per_tile + g, num, stride=n), :] = head

    def v_tile(i, w):
        y = jnp.dot(act_s[...], w, preferred_element_type=F32)
        for g in range(per_tile):
            head = y[:, g * hd : (g + 1) * hd]
            msg_s[i * per_tile + g, :, tall + new : tall + 2 * new, :] = head.reshape(pairs, new, hd).astype(BF16)
            vmix_s[pl.ds(i * per_tile + g, num, stride=n), :] = head

    stream(wq_hbm, q_tile)
    stream(wk_hbm, k_tile)
    stream(wv_hbm, v_tile)

    def msg_copy(to):
        return pltpu.make_async_remote_copy(
            src_ref=msg_s.at[to, pl.ds(home, AWAY)], dst_ref=msg_r.at[me], send_sem=msg_ss.at[to], recv_sem=msg_rs.at[me],
            device_id={"x": to}, device_id_type=MESH,
        )

    def msg_arrival(source):
        return pltpu.make_async_remote_copy(
            src_ref=msg_s.at[source, pl.ds(home, AWAY)], dst_ref=msg_r.at[source], send_sem=msg_ss.at[source],
            recv_sem=msg_rs.at[source], device_id={"x": source}, device_id_type=MESH,
        )

    def o_copy(to):
        return pltpu.make_async_remote_copy(
            src_ref=o_s.at[to], dst_ref=o_r.at[me, pl.ds(home, AWAY)], send_sem=o_ss.at[to], recv_sem=o_rs.at[me],
            device_id={"x": to}, device_id_type=MESH,
        )

    def o_arrival(source):
        return pltpu.make_async_remote_copy(
            src_ref=o_s.at[source], dst_ref=o_r.at[source, pl.ds(home, AWAY)], send_sem=o_ss.at[source], recv_sem=o_rs.at[source],
            device_id={"x": source}, device_id_type=MESH,
        )

    def kv_load(o, slot):
        first = peer(o) * rows + home * PAIR
        return (
            pltpu.make_async_copy(k_hbm.at[pl.ds(first, AWAY * PAIR)], kbuf.at[slot], ksem.at[slot]),
            pltpu.make_async_copy(v_hbm.at[pl.ds(first, AWAY * PAIR)], vbuf.at[slot], vsem.at[slot]),
        )

    for c in kv_load(0, 0):
        c.start()
    for c in own:
        c.start()
    for o in range(1, n):
        msg_copy(peer(o)).start()
    for r in range(2, AHEAD):
        bulk(r)
    msg_r[me] = msg_s[me, home:pairs]
    knew_ref[...] = kmix_s[...].reshape(rows, steps, n, hd).astype(BF16)
    vnew_ref[...] = vmix_s[...].reshape(rows, steps, n, hd).astype(BF16)

    scale = hd ** -0.5
    nt = (((1,), (1,)), ((), ()))
    r_new = lax.broadcasted_iota(jnp.int32, (tall, new), 0) % new
    c_new = lax.broadcasted_iota(jnp.int32, (tall, new), 1)
    new_ok = (c_new // steps == r_new // steps) & (c_new % steps <= r_new % steps)
    in_pair = (lax.broadcasted_iota(jnp.int32, (tall, slots), 0) % new) // steps
    in_pair_o = (lax.broadcasted_iota(jnp.int32, (tall, hd), 0) % new) // steps
    t = lax.broadcasted_iota(jnp.int32, (tall, slots), 1)

    def attend(msg, keys, values, first):
        q = msg[0:tall]
        v_new = msg[tall + new : tall + 2 * new]
        fresh = lax.dot_general(q, msg[tall : tall + new], nt, preferred_element_type=F32)
        fresh = jnp.where(new_ok, fresh * scale, -jnp.inf)
        old = lax.dot_general(q, keys(0), nt, preferred_element_type=F32)
        start = jnp.full((tall, slots), pos_ref[first], jnp.int32)
        for e in range(1, PAIR):
            other = lax.dot_general(q, keys(e), nt, preferred_element_type=F32)
            old = jnp.where(in_pair == e, other, old)
            start = jnp.where(in_pair == e, pos_ref[first + e], start)
        old = jnp.where(t < start, old * scale, -jnp.inf)
        peak = jnp.maximum(jnp.max(old, axis=-1, keepdims=True), jnp.max(fresh, axis=-1, keepdims=True))
        old = jnp.exp(old - peak)
        fresh = jnp.exp(fresh - peak)
        total = jnp.sum(old, axis=-1, keepdims=True) + jnp.sum(fresh, axis=-1, keepdims=True)
        weights = old.astype(BF16)
        mixed = jnp.dot(weights, values(0), preferred_element_type=F32)
        for e in range(1, PAIR):
            other = jnp.dot(weights, values(e), preferred_element_type=F32)
            mixed = jnp.where(in_pair_o == e, other, mixed)
        mixed = mixed + jnp.dot(fresh.astype(BF16), v_new, preferred_element_type=F32)
        return (mixed / total).astype(BF16)

    @pl.loop(0, n)
    def _(o):
        slot = lax.rem(o, 2)
        source = peer(o)

        @pl.when(o + 1 < n)
        def _():
            for c in kv_load(o + 1, 1 - slot):
                c.start()

        for c in kv_load(o, slot):
            c.wait()

        @pl.when(o > 0)
        def _():
            msg_arrival(source).wait_recv()

        for i in range(AWAY):
            o_s[source, i] = attend(
                msg_r[source, i], lambda e: kbuf[slot, i * PAIR + e], lambda e: vbuf[slot, i * PAIR + e],
                source * rows + (home + i) * PAIR,
            )

        @pl.when(o == 0)
        def _():
            o_r[me, home:pairs] = o_s[me]

        @pl.when(o > 0)
        def _():
            o_copy(source).start()

    for c in own:
        c.wait()

    def place(r):
        for src, dst in ((rk, ka_ref), (rv, va_ref)):
            @pl.loop(0, PAIR)
            def _(e):
                for h in range(n):
                    mix_s[pl.ds(h, slots, stride=n), :] = src[h, r * PAIR + e].astype(F32)
                dst[r * PAIR + e] = mix_s[...].reshape(slots, n, hd).astype(BF16)

    @pl.loop(0, home)
    def _(r):
        bulk_wait(r)

        @pl.when(r + AHEAD < pairs)
        def _():
            bulk(r + AHEAD)

        place(r)

        @pl.loop(0, n)
        def _(h):
            o_r[h, r] = attend(
                msg_s[h, r], lambda e: rk[h, r * PAIR + e], lambda e: rv[h, r * PAIR + e], me * rows + r * PAIR
            )

    for r in range(home + AHEAD, pairs):
        bulk(r)
    for o in range(1, n):
        o_arrival(peer(o)).wait_recv()
    for h in range(n):
        both = o_r[h].astype(F32)
        for j in range(q_per):
            head = both[:, j * new : (j + 1) * new, :].reshape(num, hd)
            act_s[:, (h * q_per + j) * hd : (h * q_per + j + 1) * hd] = head.astype(BF16)

    def wo_tile(i, w):
        at = pl.ds(pl.multiple_of(i * TILE, TILE), TILE)
        y = jnp.dot(act_s[...], w, preferred_element_type=F32)
        x1_s[:, at] = (hid_s[:, at] + y).astype(BF16).astype(F32)

    stream(wo_hbm, wo_tile)
    act_s[...] = rms(x1_s[...], mn_ref[...].astype(F32).reshape(1, dim)).astype(BF16)
    acc_s[...] = jnp.zeros_like(acc_s)
    tiles = wg_hbm.shape[1] // TILE

    def mlp_loads(i, slot):
        at = pl.ds(pl.multiple_of(i * TILE, TILE), TILE)
        return (
            load(cols(wg_hbm, i), wbuf, wsem, slot),
            load(cols(wu_hbm, i), ubuf, usem, slot),
            load(wd_hbm.at[at, :], dbuf, dsem, slot),
        )

    for c in mlp_loads(0, 0):
        c.start()

    @pl.loop(0, tiles)
    def _(i):
        slot = lax.rem(i, 2)

        @pl.when(i + 1 < tiles)
        def _():
            for c in mlp_loads(i + 1, 1 - slot):
                c.start()

        for c in mlp_loads(i, slot):
            c.wait()
        z = act_s[...]
        gate = jnp.dot(z, wbuf[slot], preferred_element_type=F32)
        up = jnp.dot(z, ubuf[slot], preferred_element_type=F32)
        g = (jax.nn.silu(gate) * up).astype(BF16)
        acc_s[...] += jnp.dot(g, dbuf[slot], preferred_element_type=F32)

    for c in range(0, dim, hd):
        tmp_s[...] = x1_s[:, c : c + hd] + acc_s[:, c : c + hd]
        for s in range(steps):
            out_ref[s, :, c : c + hd] = tmp_s[pl.ds(s, rows, stride=steps), :].astype(BF16)

    for o in range(1, n):
        msg_copy(peer(o)).wait_send()
        o_copy(peer(o)).wait_send()

    @pl.loop(home, pairs)
    def _(r):
        bulk_wait(r)
        place(r)

    for which, dst in enumerate((rk, rv)):
        whole = dst.at[pl.ds(0, n - 1)]
        pltpu.make_async_copy(whole, whole, bulk_s.at[which]).wait()


def store_kernel(pos_ref, hid_ref, ka_ref, va_ref, kn_ref, vn_ref, out_hbm, ko_hbm, vo_hbm, hid_sem, big, small):
    rows, steps = kn_ref.shape[0], kn_ref.shape[1]
    first = lax.axis_index("x") * rows
    sides = ((ka_ref, kn_ref, ko_hbm), (va_ref, vn_ref, vo_hbm))

    def whole(i, b):
        return pltpu.make_async_copy(sides[i][0].at[b], sides[i][2].at[b], big.at[i, b])

    def fresh(i, b):
        return pltpu.make_async_copy(sides[i][1].at[b], sides[i][2].at[b, pl.ds(pos_ref[first + b], steps)], small.at[i, b])

    hidden = pltpu.make_async_copy(hid_ref, out_hbm, hid_sem)
    for b in range(rows):
        for i in range(2):
            whole(i, b).start()
    hidden.start()
    for b in range(rows):
        for i in range(2):
            whole(i, b).wait()
            fresh(i, b).start()
    for b in range(rows):
        for i in range(2):
            fresh(i, b).wait()
    hidden.wait()


def solution(mesh):
    row_spec = P(None, ("dp", "x"), None)
    cache_in = P("dp", None, "x", None)
    cache_out = P(("dp", "x"), None, None, None)
    n = mesh.shape["x"]

    def local_run(start_pos, hidden_in, k_heads, v_heads, attn_norm, w_q, w_k, w_v, q_norm, k_norm, w_o, mlp_norm, w_gate, w_up, w_down):
        steps, rows, dim = hidden_in.shape
        slots, hd = k_heads.shape[1], k_heads.shape[3]
        heads = w_q.shape[1] // hd
        num = steps * rows
        pairs = rows // PAIR
        half = hd // 2
        inv_freq = np.power(np.float32(THETA), -np.arange(half, dtype=np.float32) * np.float32(2.0) / np.float32(hd))
        freq = jnp.asarray(np.concatenate([inv_freq, inv_freq])[None, :], F32)
        vmem = pl.BlockSpec(memory_space=pltpu.VMEM)
        hbm = pl.BlockSpec(memory_space=pltpu.HBM)
        smem = pl.BlockSpec(memory_space=pltpu.SMEM)
        tall, new = PAIR * steps * (heads // n), PAIR * steps
        dma = pltpu.SemaphoreType.DMA
        cache = (rows, slots, n, hd)
        fresh = (rows, steps, n, hd)
        blocks = pltpu.VMEM((n, rows, slots, hd), BF16)
        chunk = pltpu.VMEM((2, AWAY * PAIR, slots, hd), BF16)
        wide = pltpu.VMEM((num, dim), F32)
        head = pltpu.VMEM((num, hd), F32)
        arrived = [pltpu.VMEM(hidden_in.shape, BF16), pltpu.VMEM(fresh, BF16), pltpu.VMEM(fresh, BF16), pltpu.VMEM(cache, BF16), pltpu.VMEM(cache, BF16)]
        out, k_new, v_new, k_all, v_all = pl.pallas_call(
            functools.partial(layer_kernel, n, steps, rows, heads, hd),
            name="layer",
            out_shape=tuple(arrived),
            in_specs=[smem, vmem, vmem, hbm, hbm, vmem, hbm, hbm, hbm, vmem, vmem, hbm, vmem, hbm, hbm, hbm],
            out_specs=(vmem,) * 5,
            scratch_shapes=[
                wide, pltpu.VMEM((num, dim), BF16), wide, wide, head, head, head,
                pltpu.VMEM((n, pairs, tall + 2 * new, hd), BF16), pltpu.VMEM((n, AWAY, tall + 2 * new, hd), BF16),
                pltpu.VMEM((n, AWAY, tall, hd), BF16), pltpu.VMEM((n, pairs, tall, hd), BF16),
                blocks, blocks, chunk, chunk,
                pltpu.VMEM((2, dim, TILE), BF16), pltpu.VMEM((2, dim, TILE), BF16), pltpu.VMEM((2, TILE, dim), BF16),
                pltpu.VMEM((slots * n, hd), F32), pltpu.VMEM((num * n, hd), F32), pltpu.VMEM((num * n, hd), F32),
                dma((2,)), dma((2,)), dma((2,)), dma((2,)), dma((2,)), dma((2,)),
                dma((n,)), dma((n,)), dma((n,)), dma((n,)), dma((2,)), dma((pairs,)), dma((pairs,)),
            ],
            compiler_params=pltpu.CompilerParams(collective_id=0, has_side_effects=True, vmem_limit_bytes=VMEM_LIMIT),
        )(
            start_pos, freq, hidden_in, k_heads.reshape(-1, slots, hd), v_heads.reshape(-1, slots, hd), attn_norm,
            w_q, w_k, w_v, q_norm.reshape(1, -1), k_norm.reshape(1, -1), w_o, mlp_norm, w_gate, w_up, w_down,
        )
        return pl.pallas_call(
            store_kernel,
            name="store",
            out_shape=(jax.ShapeDtypeStruct(hidden_in.shape, BF16), jax.ShapeDtypeStruct(cache, BF16), jax.ShapeDtypeStruct(cache, BF16)),
            in_specs=[smem] + [vmem] * 5,
            out_specs=(hbm,) * 3,
            scratch_shapes=[dma, dma((2, rows)), dma((2, rows))],
            compiler_params=pltpu.CompilerParams(vmem_limit_bytes=2**20),
        )(start_pos, out, k_all, v_all, k_new, v_new)

    return jax.shard_map(local_run, mesh=mesh, in_specs=(P("dp"), row_spec, cache_in, cache_in) + (P(),) * 11, out_specs=(row_spec, cache_out, cache_out), check_vma=False)
```

time: 225 us -> 201 us (0.89)
  Pallas kernels: 216 us -> 200 us
  local copies, waits for them, and re-layouts: 7.75 us -> 0.01 us
    pallas_call x1, Pallas kernels: 18.9 us -> 7.51 us  [local_run(): pl.pallas_call(store_kernel, name='store', out_shape=(jax.ShapeDtypeStruc...]
    pallas_call x1, Pallas kernels: 197 us -> 192 us  [local_run(): pl.pallas_call(functools.partial(layer_kernel, n, steps, rows, heads, hd)...]
    unnamed x5 -> x2, local copies, waits for them, and re-layouts: 3.86 us -> 0.01 us
    reshape x2 -> x0, local copies, waits for them, and re-layouts: 2.58 us -> none  [the longest x1 1.29 us: local_run(): attn_norm.reshape(1, -1)]
where the time goes in v2:
time: 201 us
  Pallas kernels  200 us (100%)
    pallas_call x1, Pallas kernels, local_run(): pl.pallas_call(functools.partial(layer_kernel, n, steps, rows, heads, hd)...  192 us
    pallas_call x1, Pallas kernels, local_run(): pl.pallas_call(store_kernel, name='store', out_shape=(jax.ShapeDtypeStruc...  7.51 us

profile of v2, /device:TPU:81, one launch (start us, length us, event | category | flops | bytes accessed | tf_op | source)
XLA Modules:
  0.0 200.6 jit_solution(2735922903713633935)
XLA Ops:
  0.6 0.0 copy-start
  0.6 192.5 %layer.1 = (bf16[4,16,2048]{2,1,0:T(8,128)(2,1)S(1)}, bf16[16,4,8,128]{3,2,1,0:T(8,128)(2,1)S(1)}, bf16[16,4,8,128]{3,2,1,0:T(8,128)(2,1)S(1)}, bf16[16,256,8,12...) custom-call(s32[128]{0:T(128)} %pos_ref.3, f32[1,128]{1,0:T(1,128)} %constant.2.clone.freq_ref, ...), custom_call_target="tpu_custom_call" | custom-call | tf_op jit(solution)/shard_map/layer/pallas_call | solution.py:404
  193.1 0.0 copy-done
  193.1 7.5 %store.1 = (bf16[4,16,2048]{2,1,0:T(8,128)(2,1)}, bf16[16,256,8,128]{3,2,1,0:T(8,128)(2,1)}, bf16[16,256,8,128]{3,2,1,0:T(8,128)(2,1)}) custom-call(s32[128]{0:T(128)S(1)} %copy-done, bf16[4,16,2048]{2,1,0:T(8,128)(2,1)S(1)} %get-tuple-element.8.hid_ref, bf16[16,256,8,128]{3,2,1,0:T(8,128)(2,1)S(1)} %get-tuple-element.9.ka_ref, ...), custom_call_target="tpu_custom_call" | custom-call | tf_op jit(solution)/shard_map/store/pallas_call | solution.py:425
Async XLA Ops:
  0.6 192.5 %copy-start = (s32[128]{0:T(128)S(1)}, s32[128]{0:T(128)}, u32[]{:S(2)}) copy-start(s32[128]{0:T(128)} %pos_ref.3) | copy-start | bytes 1540

commit v3 on v2

--- a/solution.py
+++ b/solution.py
@@ -27,11 +27,11 @@
 
 def layer_kernel(
     n, steps, rows, heads, hd,
-    pos_ref, freq_ref, hid_ref, k_hbm, v_hbm, an_ref, wq_hbm, wk_hbm, wv_hbm, qn_ref, kn_ref, wo_hbm, mn_ref,
+    pos_ref, freq_hbm, hid_hbm, k_hbm, v_hbm, an_hbm, wq_hbm, wk_hbm, wv_hbm, qn_hbm, kn_hbm, wo_hbm, mn_hbm,
     wg_hbm, wu_hbm, wd_hbm,
     out_ref, knew_ref, vnew_ref, ka_ref, va_ref,
-    hid_s, act_s, x1_s, acc_s, tmp_s, cs_s, sn_s, msg_s, msg_r, o_s, o_r, rk, rv, kbuf, vbuf, wbuf, ubuf, dbuf, mix_s, kmix_s, vmix_s,
-    wsem, usem, dsem, ksem, vsem, own_sem, msg_ss, msg_rs, o_ss, o_rs, bulk_s, krs, vrs,
+    freq_ref, hid_ref, an_ref, qn_ref, kn_ref, mn_ref, hid_s, act_s, x1_s, acc_s, tmp_s, cs_s, sn_s, msg_s, msg_r, o_s, o_r, rk, rv, kbuf, vbuf, wbuf, ubuf, dbuf, mix_s, kmix_s, vmix_s,
+    wsem, usem, dsem, ksem, vsem, own_sem, msg_ss, msg_rs, o_ss, o_rs, bulk_s, krs, vrs, in_sem,
 ):
     me = lax.axis_index("x")
     num = steps * rows
@@ -49,24 +49,57 @@
 
     for o in range(1, n):
         pl.semaphore_signal(barrier, inc=1, device_id={"x": peer(o)}, device_id_type=MESH)
+
+    small = [
+        pltpu.make_async_copy(src, dst, in_sem.at[i])
+        for i, (src, dst) in enumerate((
+            (hid_hbm, hid_ref), (an_hbm, an_ref), (freq_hbm, freq_ref), (qn_hbm, qn_ref), (kn_hbm, kn_ref), (mn_hbm, mn_ref),
+        ))
+    ]
+    for c in small:
+        c.start()
+
+    def cols(hbm, i):
+        return hbm.at[:, pl.ds(pl.multiple_of(i * TILE, TILE), TILE)]
+
+    def load(src, dst, sem, slot):
+        return pltpu.make_async_copy(src, dst.at[slot], sem.at[slot])
+
+    load(cols(wq_hbm, 0), wbuf, wsem, 0).start()
     pl.semaphore_wait(barrier, n - 1)
 
     order = (2, 6, 4, 3, 7, 5, 1) if n == 8 else tuple(range(1, n))
 
+    def send(which, sem, first, count):
+        for o in order:
+            to = peer(o)
+            pltpu.make_async_remote_copy(
+                src_ref=(k_hbm, v_hbm)[which].at[pl.ds(to * rows + first, count)],
+                dst_ref=(rk, rv)[which].at[me, pl.ds(first, count)],
+                send_sem=bulk_s.at[which], recv_sem=(krs, vrs)[which].at[sem], device_id={"x": to}, device_id_type=MESH,
+            ).start()
+
     def bulk(r):
-        for which, (src, dst, arrived) in enumerate(((k_hbm, rk, krs), (v_hbm, rv, vrs))):
-            for o in order:
-                to = peer(o)
-                pltpu.make_async_remote_copy(
-                    src_ref=src.at[pl.ds(to * rows + r * PAIR, PAIR)],
-                    dst_ref=dst.at[me, pl.ds(r * PAIR, PAIR)],
-                    send_sem=bulk_s.at[which], recv_sem=arrived.at[r], device_id={"x": to}, device_id_type=MESH,
-                ).start()
-
-    def bulk_wait(r):
-        for dst, arrived in ((rk, krs), (rv, vrs)):
-            whole = dst.at[pl.ds(0, n - 1), pl.ds(0, PAIR)]
-            pltpu.make_async_copy(whole, whole, arrived.at[r]).wait()
+        send(0, r, r * PAIR, PAIR)
+        send(1, r, r * PAIR, PAIR)
+
+    def bulk_last():
+        send(0, pairs - 1, rows - PAIR, PAIR)
+        for e in range(PAIR):
+            send(1, pairs - 1 + e, rows - PAIR + e, 1)
+
+    def bulk_next(r):
+        @pl.when(r < pairs - 1)
+        def _():
+            bulk(r)
+
+        @pl.when(r == pairs - 1)
+        def _():
+            bulk_last()
+
+    def bulk_wait(which, r, count=PAIR):
+        whole = (rk, rv)[which].at[pl.ds(0, n - 1), pl.ds(0, count)]
+        pltpu.make_async_copy(whole, whole, (krs, vrs)[which].at[r]).wait()
 
     for r in range(2):
         bulk(r)
@@ -76,15 +109,10 @@
         pltpu.make_async_copy(v_hbm.at[pl.ds(me * rows, rows)], rv.at[me], own_sem.at[1]),
     ]
 
-    def cols(hbm, i):
-        return hbm.at[:, pl.ds(pl.multiple_of(i * TILE, TILE), TILE)]
-
-    def load(src, dst, sem, slot):
-        return pltpu.make_async_copy(src, dst.at[slot], sem.at[slot])
-
-    def stream(hbm, body):
+    def stream(hbm, body, started=False):
         tiles = hbm.shape[1] // TILE
-        load(cols(hbm, 0), wbuf, wsem, 0).start()
+        if not started:
+            load(cols(hbm, 0), wbuf, wsem, 0).start()
 
         @pl.loop(0, tiles)
         def _(i):
@@ -97,6 +125,8 @@
             load(cols(hbm, i), wbuf, wsem, slot).wait()
             body(i, wbuf[slot])
 
+    for c in small:
+        c.wait()
     for c in range(0, dim, hd):
         for s in range(steps):
             tmp_s[pl.ds(s, rows, stride=steps), :] = hid_ref[s, :, c : c + hd].astype(F32)
@@ -143,7 +173,7 @@
             msg_s[i * per_tile + g, :, tall + new : tall + 2 * new, :] = head.reshape(pairs, new, hd).astype(BF16)
             vmix_s[pl.ds(i * per_tile + g, num, stride=n), :] = head
 
-    stream(wq_hbm, q_tile)
+    stream(wq_hbm, q_tile, started=True)
     stream(wk_hbm, k_tile)
     stream(wv_hbm, v_tile)
 
@@ -182,13 +212,13 @@
         c.start()
     for c in own:
         c.start()
+    knew_ref[...] = kmix_s[...].reshape(rows, steps, n, hd).astype(BF16)
+    vnew_ref[...] = vmix_s[...].reshape(rows, steps, n, hd).astype(BF16)
+    msg_r[me] = msg_s[me, home:pairs]
     for o in range(1, n):
         msg_copy(peer(o)).start()
     for r in range(2, AHEAD):
         bulk(r)
-    msg_r[me] = msg_s[me, home:pairs]
-    knew_ref[...] = kmix_s[...].reshape(rows, steps, n, hd).astype(BF16)
-    vnew_ref[...] = vmix_s[...].reshape(rows, steps, n, hd).astype(BF16)
 
     scale = hd ** -0.5
     nt = (((1,), (1,)), ((), ()))
@@ -250,30 +280,30 @@
         def _():
             o_r[me, home:pairs] = o_s[me]
 
-        @pl.when(o > 0)
-        def _():
-            o_copy(source).start()
+        @pl.when(o > 1)
+        def _():
+            o_copy(peer(o - 1)).start()
 
     for c in own:
         c.wait()
-
-    def place(r):
-        for src, dst in ((rk, ka_ref), (rv, va_ref)):
-            @pl.loop(0, PAIR)
-            def _(e):
-                for h in range(n):
-                    mix_s[pl.ds(h, slots, stride=n), :] = src[h, r * PAIR + e].astype(F32)
-                dst[r * PAIR + e] = mix_s[...].reshape(slots, n, hd).astype(BF16)
+    o_copy(peer(n - 1)).start()
+
+    def place(which, first, count):
+        src, dst = ((rk, ka_ref), (rv, va_ref))[which]
+
+        @pl.loop(0, count)
+        def _(e):
+            for h in range(n):
+                mix_s[pl.ds(h, slots, stride=n), :] = src[h, first + e].astype(F32)
+            dst[first + e] = mix_s[...].reshape(slots, n, hd).astype(BF16)
 
     @pl.loop(0, home)
     def _(r):
-        bulk_wait(r)
-
-        @pl.when(r + AHEAD < pairs)
-        def _():
-            bulk(r + AHEAD)
-
-        place(r)
+        bulk_wait(0, r)
+        bulk_wait(1, r)
+        bulk_next(r + AHEAD)
+        place(0, r * PAIR, PAIR)
+        place(1, r * PAIR, PAIR)
 
         @pl.loop(0, n)
         def _(h):
@@ -281,8 +311,6 @@
                 msg_s[h, r], lambda e: rk[h, r * PAIR + e], lambda e: rv[h, r * PAIR + e], me * rows + r * PAIR
             )
 
-    for r in range(home + AHEAD, pairs):
-        bulk(r)
     for o in range(1, n):
         o_arrival(peer(o)).wait_recv()
     for h in range(n):
@@ -338,40 +366,39 @@
         msg_copy(peer(o)).wait_send()
         o_copy(peer(o)).wait_send()
 
-    @pl.loop(home, pairs)
+    @pl.loop(home, pairs - 1)
     def _(r):
-        bulk_wait(r)
-        place(r)
+        for which in range(2):
+            bulk_wait(which, r)
+            place(which, r * PAIR, PAIR)
+
+    bulk_wait(0, pairs - 1)
+    place(0, rows - PAIR, PAIR)
+    for e in range(PAIR):
+        bulk_wait(1, pairs - 1 + e, 1)
+        place(1, rows - PAIR + e, 1)
 
     for which, dst in enumerate((rk, rv)):
         whole = dst.at[pl.ds(0, n - 1)]
         pltpu.make_async_copy(whole, whole, bulk_s.at[which]).wait()
 
 
-def store_kernel(pos_ref, hid_ref, ka_ref, va_ref, kn_ref, vn_ref, out_hbm, ko_hbm, vo_hbm, hid_sem, big, small):
+def store_kernel(pos_ref, hid_ref, ka_in, va_in, kn_ref, vn_ref, out_hbm, ko_hbm, vo_hbm, ka_ref, va_ref, hid_sem, sems):
     rows, steps = kn_ref.shape[0], kn_ref.shape[1]
     first = lax.axis_index("x") * rows
-    sides = ((ka_ref, kn_ref, ko_hbm), (va_ref, vn_ref, vo_hbm))
-
-    def whole(i, b):
-        return pltpu.make_async_copy(sides[i][0].at[b], sides[i][2].at[b], big.at[i, b])
-
-    def fresh(i, b):
-        return pltpu.make_async_copy(sides[i][1].at[b], sides[i][2].at[b, pl.ds(pos_ref[first + b], steps)], small.at[i, b])
-
-    hidden = pltpu.make_async_copy(hid_ref, out_hbm, hid_sem)
     for b in range(rows):
-        for i in range(2):
-            whole(i, b).start()
-    hidden.start()
+        at = pos_ref[first + b]
+        for s in range(steps):
+            ka_ref[b, at + s] = kn_ref[b, s]
+            va_ref[b, at + s] = vn_ref[b, s]
+    copies = [pltpu.make_async_copy(hid_ref, out_hbm, hid_sem)]
     for b in range(rows):
-        for i in range(2):
-            whole(i, b).wait()
-            fresh(i, b).start()
-    for b in range(rows):
-        for i in range(2):
-            fresh(i, b).wait()
-    hidden.wait()
+        copies.append(pltpu.make_async_copy(ka_ref.at[b], ko_hbm.at[b], sems.at[0, b]))
+        copies.append(pltpu.make_async_copy(va_ref.at[b], vo_hbm.at[b], sems.at[1, b]))
+    for c in copies:
+        c.start()
+    for c in copies:
+        c.wait()
 
 
 def solution(mesh):
@@ -405,9 +432,11 @@
             functools.partial(layer_kernel, n, steps, rows, heads, hd),
             name="layer",
             out_shape=tuple(arrived),
-            in_specs=[smem, vmem, vmem, hbm, hbm, vmem, hbm, hbm, hbm, vmem, vmem, hbm, vmem, hbm, hbm, hbm],
+            in_specs=[smem] + [hbm] * 15,
             out_specs=(vmem,) * 5,
             scratch_shapes=[
+                pltpu.VMEM(freq.shape, F32), pltpu.VMEM(hidden_in.shape, BF16), pltpu.VMEM((dim,), BF16),
+                pltpu.VMEM((1, hd), BF16), pltpu.VMEM((1, hd), BF16), pltpu.VMEM((dim,), BF16),
                 wide, pltpu.VMEM((num, dim), BF16), wide, wide, head, head, head,
                 pltpu.VMEM((n, pairs, tall + 2 * new, hd), BF16), pltpu.VMEM((n, AWAY, tall + 2 * new, hd), BF16),
                 pltpu.VMEM((n, AWAY, tall, hd), BF16), pltpu.VMEM((n, pairs, tall, hd), BF16),
@@ -415,7 +444,7 @@
                 pltpu.VMEM((2, dim, TILE), BF16), pltpu.VMEM((2, dim, TILE), BF16), pltpu.VMEM((2, TILE, dim), BF16),
                 pltpu.VMEM((slots * n, hd), F32), pltpu.VMEM((num * n, hd), F32), pltpu.VMEM((num * n, hd), F32),
                 dma((2,)), dma((2,)), dma((2,)), dma((2,)), dma((2,)), dma((2,)),
-                dma((n,)), dma((n,)), dma((n,)), dma((n,)), dma((2,)), dma((pairs,)), dma((pairs,)),
+                dma((n,)), dma((n,)), dma((n,)), dma((n,)), dma((2,)), dma((pairs,)), dma((pairs - 1 + PAIR,)), dma((6,)),
             ],
             compiler_params=pltpu.CompilerParams(collective_id=0, has_side_effects=True, vmem_limit_bytes=VMEM_LIMIT),
         )(
@@ -425,11 +454,15 @@
         return pl.pallas_call(
             store_kernel,
             name="store",
-            out_shape=(jax.ShapeDtypeStruct(hidden_in.shape, BF16), jax.ShapeDtypeStruct(cache, BF16), jax.ShapeDtypeStruct(cache, BF16)),
+            out_shape=(
+                jax.ShapeDtypeStruct(hidden_in.shape, BF16), jax.ShapeDtypeStruct(cache, BF16), jax.ShapeDtypeStruct(cache, BF16),
+                pltpu.VMEM(cache, BF16), pltpu.VMEM(cache, BF16),
+            ),
             in_specs=[smem] + [vmem] * 5,
-            out_specs=(hbm,) * 3,
-            scratch_shapes=[dma, dma((2, rows)), dma((2, rows))],
+            out_specs=(hbm,) * 3 + (vmem,) * 2,
+            input_output_aliases={2: 3, 3: 4},
+            scratch_shapes=[dma, dma((2, rows))],
             compiler_params=pltpu.CompilerParams(vmem_limit_bytes=2**20),
-        )(start_pos, out, k_all, v_all, k_new, v_new)
+        )(start_pos, out, k_all, v_all, k_new, v_new)[:3]
 
     return jax.shard_map(local_run, mesh=mesh, in_specs=(P("dp"), row_spec, cache_in, cache_in) + (P(),) * 11, out_specs=(row_spec, cache_out, cache_out), check_vma=False)

time: 201 us -> 199 us (0.990)
  no operation moved by 1% of the time
where the time goes in v3:
time: 199 us
  Pallas kernels  198 us (99%)
    pallas_call x1, Pallas kernels, local_run(): pl.pallas_call(functools.partial(layer_kernel, n, steps, rows, heads, hd)...  191 us
    pallas_call x1, Pallas kernels, local_run(): pl.pallas_call(store_kernel, name='store', out_shape=(jax.ShapeDtypeStruc...  6.79 us

profile of v3, /device:TPU:81, one launch (start us, length us, event | category | flops | bytes accessed | tf_op | source)
XLA Modules:
  0.0 198.7 jit_solution(16123212777722066246)
XLA Ops:
  0.6 0.0 copy-start
  0.6 191.2 %layer.1 = (bf16[4,16,2048]{2,1,0:T(8,128)(2,1)S(1)}, bf16[16,4,8,128]{3,2,1,0:T(8,128)(2,1)S(1)}, bf16[16,4,8,128]{3,2,1,0:T(8,128)(2,1)S(1)}, bf16[16,256,8,12...) custom-call(s32[128]{0:T(128)} %pos_ref.3, f32[1,128]{1,0:T(1,128)} %constant.2.clone.freq_hbm, ...), custom_call_target="tpu_custom_call" | custom-call | tf_op jit(solution)/shard_map/layer/pallas_call | solution.py:431
  191.9 0.0 copy-done
  191.9 6.8 %store.1 = (bf16[4,16,2048]{2,1,0:T(8,128)(2,1)}, bf16[16,256,8,128]{3,2,1,0:T(8,128)(2,1)}, bf16[16,256,8,128]{3,2,1,0:T(8,128)(2,1)}, bf16[16,256,8,128]{3,2,1...) custom-call(s32[128]{0:T(128)S(1)} %copy-done, ...), custom_call_target="tpu_custom_call", output_to_operand_aliasing={{3}: (2, {}), {4}: (3, {})} | custom-call | tf_op jit(solution)/shard_map/store/pallas_call | solution.py:454
Async XLA Ops:
  0.6 191.2 %copy-start = (s32[128]{0:T(128)S(1)}, s32[128]{0:T(128)}, u32[]{:S(2)}) copy-start(s32[128]{0:T(128)} %pos_ref.3) | copy-start | bytes 1540

commit v4 on v3

--- a/solution.py
+++ b/solution.py
@@ -15,7 +15,7 @@
 MESH = pl.DeviceIdType.MESH
 TILE = 512
 PAIR = 2
-AWAY = 3
+AWAY = 2
 VMEM_LIMIT = 44 * 2**20
 AHEAD = 4
 

time: 199 us -> 198 us (level)
  no operation moved by 1% of the time
where the time goes in v4:
time: 198 us
  Pallas kernels  197 us (99%)
    pallas_call x1, Pallas kernels, local_run(): pl.pallas_call(functools.partial(layer_kernel, n, steps, rows, heads, hd)...  190 us
    pallas_call x1, Pallas kernels, local_run(): pl.pallas_call(store_kernel, name='store', out_shape=(jax.ShapeDtypeStruc...  6.79 us

profile of v4, /device:TPU:81, one launch (start us, length us, event | category | flops | bytes accessed | tf_op | source)
XLA Modules:
  0.0 197.6 jit_solution(7227610103724421928)
XLA Ops:
  0.6 0.0 copy-start
  0.6 190.2 %layer.1 = (bf16[4,16,2048]{2,1,0:T(8,128)(2,1)S(1)}, bf16[16,4,8,128]{3,2,1,0:T(8,128)(2,1)S(1)}, bf16[16,4,8,128]{3,2,1,0:T(8,128)(2,1)S(1)}, bf16[16,256,8,12...) custom-call(s32[128]{0:T(128)} %pos_ref.3, f32[1,128]{1,0:T(1,128)} %constant.2.clone.freq_hbm, ...), custom_call_target="tpu_custom_call" | custom-call | tf_op jit(solution)/shard_map/layer/pallas_call | solution.py:431
  190.8 0.0 copy-done
  190.8 6.8 %store.1 = (bf16[4,16,2048]{2,1,0:T(8,128)(2,1)}, bf16[16,256,8,128]{3,2,1,0:T(8,128)(2,1)}, bf16[16,256,8,128]{3,2,1,0:T(8,128)(2,1)}, bf16[16,256,8,128]{3,2,1...) custom-call(s32[128]{0:T(128)S(1)} %copy-done, ...), custom_call_target="tpu_custom_call", output_to_operand_aliasing={{3}: (2, {}), {4}: (3, {})} | custom-call | tf_op jit(solution)/shard_map/store/pallas_call | solution.py:454
Async XLA Ops:
  0.6 190.2 %copy-start = (s32[128]{0:T(128)S(1)}, s32[128]{0:T(128)}, u32[]{:S(2)}) copy-start(s32[128]{0:T(128)} %pos_ref.3) | copy-start | bytes 1540

commit v5 on v4

--- a/solution.py
+++ b/solution.py
@@ -31,7 +31,7 @@
     wg_hbm, wu_hbm, wd_hbm,
     out_ref, knew_ref, vnew_ref, ka_ref, va_ref,
     freq_ref, hid_ref, an_ref, qn_ref, kn_ref, mn_ref, hid_s, act_s, x1_s, acc_s, tmp_s, cs_s, sn_s, msg_s, msg_r, o_s, o_r, rk, rv, kbuf, vbuf, wbuf, ubuf, dbuf, mix_s, kmix_s, vmix_s,
-    wsem, usem, dsem, ksem, vsem, own_sem, msg_ss, msg_rs, o_ss, o_rs, bulk_s, krs, vrs, in_sem,
+    wsem, usem, dsem, ksem, vsem, own_sem, msg_ss, msg_rs, o_ss, o_rs, bulk_s, krs, vrs, in_sem, ready,
 ):
     me = lax.axis_index("x")
     num = steps * rows
@@ -44,11 +44,19 @@
     new = PAIR * steps
     barrier = pltpu.get_barrier_semaphore()
 
+    chips = n // 2
+    chip, core = me // 2, lax.rem(me, 2)
+
     def peer(o):
         return lax.rem(me + o, n)
 
-    for o in range(1, n):
-        pl.semaphore_signal(barrier, inc=1, device_id={"x": peer(o)}, device_id_type=MESH)
+    def away(hops, cross):
+        return lax.rem(chip + hops, chips) * 2 + (1 - core if cross else core)
+
+    near = [(0, True)] + [(hops, cross) for hops in (1, chips - 1) for cross in (False, True)]
+    far = [(hops, cross) for hops in range(2, chips - 1) for cross in (False, True)]
+    for to in near:
+        pl.semaphore_signal(barrier, inc=1, device_id={"x": away(*to)}, device_id_type=MESH)
 
     small = [
         pltpu.make_async_copy(src, dst, in_sem.at[i])
@@ -66,27 +74,32 @@
         return pltpu.make_async_copy(src, dst.at[slot], sem.at[slot])
 
     load(cols(wq_hbm, 0), wbuf, wsem, 0).start()
-    pl.semaphore_wait(barrier, n - 1)
-
-    order = (2, 6, 4, 3, 7, 5, 1) if n == 8 else tuple(range(1, n))
-
-    def send(which, sem, first, count):
-        for o in order:
-            to = peer(o)
+    pl.semaphore_wait(barrier, len(near))
+    pl.semaphore_signal(ready, inc=1, device_id={"x": away(chips - 1, False)}, device_id_type=MESH)
+
+    def send(which, sem, first, count, lo, size, order):
+        for hops, cross in order:
+            to = away(hops, cross)
             pltpu.make_async_remote_copy(
-                src_ref=(k_hbm, v_hbm)[which].at[pl.ds(to * rows + first, count)],
-                dst_ref=(rk, rv)[which].at[me, pl.ds(first, count)],
+                src_ref=(k_hbm, v_hbm)[which].at[pl.ds(to * rows + first, count), pl.ds(lo, size)],
+                dst_ref=(rk, rv)[which].at[me, pl.ds(first, count), pl.ds(lo, size)],
                 send_sem=bulk_s.at[which], recv_sem=(krs, vrs)[which].at[sem], device_id={"x": to}, device_id_type=MESH,
             ).start()
 
+    mixed_order = [(1, False), (chips - 1, False)] + far[:1] + [(1, True), (chips - 1, True)] + far[1:] + [(0, True)]
+    far_first = far + [(1, False), (chips - 1, False), (1, True), (chips - 1, True), (0, True)]
+    last = [(0, pairs - 1, rows - PAIR, PAIR, 0, slots)]
+    last += [(1, pairs - 1 + e, rows - PAIR + e, 1, 0, slots) for e in range(PAIR - 1)]
+    for i, (lo, size) in enumerate(((0, slots // 2), (slots // 2, slots // 4), (slots * 3 // 4, slots // 4))):
+        last.append((1, pairs - 2 + PAIR + i, rows - 1, 1, lo, size))
+
     def bulk(r):
-        send(0, r, r * PAIR, PAIR)
-        send(1, r, r * PAIR, PAIR)
+        send(0, r, r * PAIR, PAIR, 0, slots, mixed_order)
+        send(1, r, r * PAIR, PAIR, 0, slots, mixed_order)
 
     def bulk_last():
-        send(0, pairs - 1, rows - PAIR, PAIR)
-        for e in range(PAIR):
-            send(1, pairs - 1 + e, rows - PAIR + e, 1)
+        for which, sem, first, count, lo, size in last:
+            send(which, sem, first, count, lo, size, far_first)
 
     def bulk_next(r):
         @pl.when(r < pairs - 1)
@@ -97,12 +110,15 @@
         def _():
             bulk_last()
 
-    def bulk_wait(which, r, count=PAIR):
-        whole = (rk, rv)[which].at[pl.ds(0, n - 1), pl.ds(0, count)]
-        pltpu.make_async_copy(whole, whole, (krs, vrs)[which].at[r]).wait()
-
-    for r in range(2):
-        bulk(r)
+    def bulk_wait(which, sem, count, size):
+        whole = (rk, rv)[which].at[pl.ds(0, n - 1), pl.ds(0, count), pl.ds(0, size)]
+        pltpu.make_async_copy(whole, whole, (krs, vrs)[which].at[sem]).wait()
+
+    send(0, 0, 0, PAIR, 0, slots, near)
+    pl.semaphore_wait(ready, 1)
+    send(0, 0, 0, PAIR, 0, slots, far)
+    send(1, 0, 0, PAIR, 0, slots, mixed_order)
+    bulk(1)
 
     own = [
         pltpu.make_async_copy(k_hbm.at[pl.ds(me * rows, rows)], rk.at[me], own_sem.at[0]),
@@ -288,19 +304,19 @@
         c.wait()
     o_copy(peer(n - 1)).start()
 
-    def place(which, first, count):
+    def place(which, first, count, lo=0, size=slots):
         src, dst = ((rk, ka_ref), (rv, va_ref))[which]
 
         @pl.loop(0, count)
         def _(e):
             for h in range(n):
-                mix_s[pl.ds(h, slots, stride=n), :] = src[h, first + e].astype(F32)
-            dst[first + e] = mix_s[...].reshape(slots, n, hd).astype(BF16)
+                mix_s[pl.ds(h, size, stride=n), :] = src[h, first + e, lo : lo + size].astype(F32)
+            dst[first + e, lo : lo + size] = mix_s[0 : size * n].reshape(size, n, hd).astype(BF16)
 
     @pl.loop(0, home)
     def _(r):
-        bulk_wait(0, r)
-        bulk_wait(1, r)
+        bulk_wait(0, r, PAIR, slots)
+        bulk_wait(1, r, PAIR, slots)
         bulk_next(r + AHEAD)
         place(0, r * PAIR, PAIR)
         place(1, r * PAIR, PAIR)
@@ -369,14 +385,12 @@
     @pl.loop(home, pairs - 1)
     def _(r):
         for which in range(2):
-            bulk_wait(which, r)
+            bulk_wait(which, r, PAIR, slots)
             place(which, r * PAIR, PAIR)
 
-    bulk_wait(0, pairs - 1)
-    place(0, rows - PAIR, PAIR)
-    for e in range(PAIR):
-        bulk_wait(1, pairs - 1 + e, 1)
-        place(1, rows - PAIR + e, 1)
+    for which, sem, first, count, lo, size in last:
+        bulk_wait(which, sem, count, size)
+        place(which, first, count, lo, size)
 
     for which, dst in enumerate((rk, rv)):
         whole = dst.at[pl.ds(0, n - 1)]
@@ -386,19 +400,27 @@
 def store_kernel(pos_ref, hid_ref, ka_in, va_in, kn_ref, vn_ref, out_hbm, ko_hbm, vo_hbm, ka_ref, va_ref, hid_sem, sems):
     rows, steps = kn_ref.shape[0], kn_ref.shape[1]
     first = lax.axis_index("x") * rows
+    hidden = pltpu.make_async_copy(hid_ref, out_hbm, hid_sem)
+    hidden.start()
+    copies = []
     for b in range(rows):
-        at = pos_ref[first + b]
-        for s in range(steps):
-            ka_ref[b, at + s] = kn_ref[b, s]
-            va_ref[b, at + s] = vn_ref[b, s]
-    copies = [pltpu.make_async_copy(hid_ref, out_hbm, hid_sem)]
-    for b in range(rows):
-        copies.append(pltpu.make_async_copy(ka_ref.at[b], ko_hbm.at[b], sems.at[0, b]))
-        copies.append(pltpu.make_async_copy(va_ref.at[b], vo_hbm.at[b], sems.at[1, b]))
-    for c in copies:
-        c.start()
-    for c in copies:
-        c.wait()
+        copies.append((
+            pltpu.make_async_copy(ka_ref.at[b], ko_hbm.at[b], sems.at[0, b]),
+            pltpu.make_async_copy(va_ref.at[b], vo_hbm.at[b], sems.at[1, b]),
+        ))
+    for b in range(rows + 1):
+        if b < rows:
+            at = pos_ref[first + b]
+            for s in range(steps):
+                ka_ref[b, at + s] = kn_ref[b, s]
+                va_ref[b, at + s] = vn_ref[b, s]
+        if b > 0:
+            for c in copies[b - 1]:
+                c.start()
+    for pair in copies:
+        for c in pair:
+            c.wait()
+    hidden.wait()
 
 
 def solution(mesh):
@@ -444,7 +466,7 @@
                 pltpu.VMEM((2, dim, TILE), BF16), pltpu.VMEM((2, dim, TILE), BF16), pltpu.VMEM((2, TILE, dim), BF16),
                 pltpu.VMEM((slots * n, hd), F32), pltpu.VMEM((num * n, hd), F32), pltpu.VMEM((num * n, hd), F32),
                 dma((2,)), dma((2,)), dma((2,)), dma((2,)), dma((2,)), dma((2,)),
-                dma((n,)), dma((n,)), dma((n,)), dma((n,)), dma((2,)), dma((pairs,)), dma((pairs - 1 + PAIR,)), dma((6,)),
+                dma((n,)), dma((n,)), dma((n,)), dma((n,)), dma((2,)), dma((pairs,)), dma((pairs + PAIR + 1,)), dma((6,)), pltpu.SemaphoreType.REGULAR,
             ],
             compiler_params=pltpu.CompilerParams(collective_id=0, has_side_effects=True, vmem_limit_bytes=VMEM_LIMIT),
         )(

time: 198 us -> 197 us (level)
  no operation moved by 1% of the time
where the time goes in v5:
time: 197 us
  Pallas kernels  196 us (99%)
    pallas_call x1, Pallas kernels, local_run(): pl.pallas_call(functools.partial(layer_kernel, n, steps, rows, heads, hd)...  190 us
    pallas_call x1, Pallas kernels, local_run(): pl.pallas_call(store_kernel, name='store', out_shape=(jax.ShapeDtypeStruc...  6.74 us

profile of v5, /device:TPU:81, one launch (start us, length us, event | category | flops | bytes accessed | tf_op | source)
XLA Modules:
  0.0 197.1 jit_solution(10029695794001125949)
XLA Ops:
  0.6 0.0 copy-start
  0.6 189.7 %layer.1 = (bf16[4,16,2048]{2,1,0:T(8,128)(2,1)S(1)}, bf16[16,4,8,128]{3,2,1,0:T(8,128)(2,1)S(1)}, bf16[16,4,8,128]{3,2,1,0:T(8,128)(2,1)S(1)}, bf16[16,256,8,12...) custom-call(s32[128]{0:T(128)} %pos_ref.3, f32[1,128]{1,0:T(1,128)} %constant.2.clone.freq_hbm, ...), custom_call_target="tpu_custom_call" | custom-call | tf_op jit(solution)/shard_map/layer/pallas_call | solution.py:453
  190.3 0.0 copy-done
  190.3 6.7 %store.1 = (bf16[4,16,2048]{2,1,0:T(8,128)(2,1)}, bf16[16,256,8,128]{3,2,1,0:T(8,128)(2,1)}, bf16[16,256,8,128]{3,2,1,0:T(8,128)(2,1)}, bf16[16,256,8,128]{3,2,1...) custom-call(s32[128]{0:T(128)S(1)} %copy-done, ...), custom_call_target="tpu_custom_call", output_to_operand_aliasing={{3}: (2, {}), {4}: (3, {})} | custom-call | tf_op jit(solution)/shard_map/store/pallas_call | solution.py:476
Async XLA Ops:
  0.6 189.7 %copy-start = (s32[128]{0:T(128)S(1)}, s32[128]{0:T(128)}, u32[]{:S(2)}) copy-start(s32[128]{0:T(128)} %pos_ref.3) | copy-start | bytes 1540

commit v6 on v5

--- a/solution.py
+++ b/solution.py
@@ -29,9 +29,9 @@
     n, steps, rows, heads, hd,
     pos_ref, freq_hbm, hid_hbm, k_hbm, v_hbm, an_hbm, wq_hbm, wk_hbm, wv_hbm, qn_hbm, kn_hbm, wo_hbm, mn_hbm,
     wg_hbm, wu_hbm, wd_hbm,
-    out_ref, knew_ref, vnew_ref, ka_ref, va_ref,
-    freq_ref, hid_ref, an_ref, qn_ref, kn_ref, mn_ref, hid_s, act_s, x1_s, acc_s, tmp_s, cs_s, sn_s, msg_s, msg_r, o_s, o_r, rk, rv, kbuf, vbuf, wbuf, ubuf, dbuf, mix_s, kmix_s, vmix_s,
-    wsem, usem, dsem, ksem, vsem, own_sem, msg_ss, msg_rs, o_ss, o_rs, bulk_s, krs, vrs, in_sem, ready,
+    out_ref, ka_ref, va_ref,
+    freq_ref, hid_ref, an_ref, qn_ref, kn_ref, mn_ref, hid_s, act_s, x1_s, acc_s, tmp_s, cs_s, sn_s, msg_s, msg_r, o_s, o_r, rk, rv, kbuf, vbuf, wbuf, ubuf, dbuf, mix_s, kmix_s, vmix_s, stage_s,
+    wsem, usem, dsem, ksem, vsem, own_sem, msg_ss, msg_rs, o_ss, o_rs, bulk_s, krs, vrs, in_sem, ready, stage_sem,
 ):
     me = lax.axis_index("x")
     num = steps * rows
@@ -73,6 +73,11 @@
     def load(src, dst, sem, slot):
         return pltpu.make_async_copy(src, dst.at[slot], sem.at[slot])
 
+    staged = [
+        pltpu.make_async_copy(k_hbm.at[away(*to) * rows], stage_s.at[i], stage_sem.at[i]) for i, to in enumerate(near[1:])
+    ]
+    for c in staged:
+        c.start()
     load(cols(wq_hbm, 0), wbuf, wsem, 0).start()
     pl.semaphore_wait(barrier, len(near))
     pl.semaphore_signal(ready, inc=1, device_id={"x": away(chips - 1, False)}, device_id_type=MESH)
@@ -114,7 +119,14 @@
         whole = (rk, rv)[which].at[pl.ds(0, n - 1), pl.ds(0, count), pl.ds(0, size)]
         pltpu.make_async_copy(whole, whole, (krs, vrs)[which].at[sem]).wait()
 
-    send(0, 0, 0, PAIR, 0, slots, near)
+    for i, to in enumerate(near[1:]):
+        staged[i].wait()
+        pltpu.make_async_remote_copy(
+            src_ref=stage_s.at[i], dst_ref=rk.at[me, 0], send_sem=bulk_s.at[0], recv_sem=krs.at[0],
+            device_id={"x": away(*to)}, device_id_type=MESH,
+        ).start()
+    send(0, 0, 1, PAIR - 1, 0, slots, near[1:])
+    send(0, 0, 0, PAIR, 0, slots, near[:1])
     pl.semaphore_wait(ready, 1)
     send(0, 0, 0, PAIR, 0, slots, far)
     send(1, 0, 0, PAIR, 0, slots, mixed_order)
@@ -228,8 +240,6 @@
         c.start()
     for c in own:
         c.start()
-    knew_ref[...] = kmix_s[...].reshape(rows, steps, n, hd).astype(BF16)
-    vnew_ref[...] = vmix_s[...].reshape(rows, steps, n, hd).astype(BF16)
     msg_r[me] = msg_s[me, home:pairs]
     for o in range(1, n):
         msg_copy(peer(o)).start()
@@ -311,7 +321,13 @@
         def _(e):
             for h in range(n):
                 mix_s[pl.ds(h, size, stride=n), :] = src[h, first + e, lo : lo + size].astype(F32)
-            dst[first + e, lo : lo + size] = mix_s[0 : size * n].reshape(size, n, hd).astype(BF16)
+            mixed = mix_s[0 : size * n].reshape(size, n, hd)
+            slot = lo + lax.broadcasted_iota(jnp.int32, (size, n, hd), 0)
+            for s in range(steps):
+                at = pl.multiple_of(((first + e) * steps + s) * n, n)
+                fresh = (kmix_s, vmix_s)[which][pl.ds(at, n), :]
+                mixed = jnp.where(slot == pos_ref[me * rows + first + e] + s, fresh[None], mixed)
+            dst[first + e, lo : lo + size] = mixed.astype(BF16)
 
     @pl.loop(0, home)
     def _(r):
@@ -397,30 +413,16 @@
         pltpu.make_async_copy(whole, whole, bulk_s.at[which]).wait()
 
 
-def store_kernel(pos_ref, hid_ref, ka_in, va_in, kn_ref, vn_ref, out_hbm, ko_hbm, vo_hbm, ka_ref, va_ref, hid_sem, sems):
-    rows, steps = kn_ref.shape[0], kn_ref.shape[1]
-    first = lax.axis_index("x") * rows
-    hidden = pltpu.make_async_copy(hid_ref, out_hbm, hid_sem)
-    hidden.start()
+def store_kernel(hid_ref, ka_ref, va_ref, out_hbm, ko_hbm, vo_hbm, hid_sem, sems):
     copies = []
-    for b in range(rows):
-        copies.append((
-            pltpu.make_async_copy(ka_ref.at[b], ko_hbm.at[b], sems.at[0, b]),
-            pltpu.make_async_copy(va_ref.at[b], vo_hbm.at[b], sems.at[1, b]),
-        ))
-    for b in range(rows + 1):
-        if b < rows:
-            at = pos_ref[first + b]
-            for s in range(steps):
-                ka_ref[b, at + s] = kn_ref[b, s]
-                va_ref[b, at + s] = vn_ref[b, s]
-        if b > 0:
-            for c in copies[b - 1]:
-                c.start()
-    for pair in copies:
-        for c in pair:
-            c.wait()
-    hidden.wait()
+    for b in range(ka_ref.shape[0]):
+        copies.append(pltpu.make_async_copy(ka_ref.at[b], ko_hbm.at[b], sems.at[0, b]))
+        copies.append(pltpu.make_async_copy(va_ref.at[b], vo_hbm.at[b], sems.at[1, b]))
+    copies.append(pltpu.make_async_copy(hid_ref, out_hbm, hid_sem))
+    for c in copies:
+        c.start()
+    for c in copies:
+        c.wait()
 
 
 def solution(mesh):
@@ -444,18 +446,17 @@
         tall, new = PAIR * steps * (heads // n), PAIR * steps
         dma = pltpu.SemaphoreType.DMA
         cache = (rows, slots, n, hd)
-        fresh = (rows, steps, n, hd)
         blocks = pltpu.VMEM((n, rows, slots, hd), BF16)
         chunk = pltpu.VMEM((2, AWAY * PAIR, slots, hd), BF16)
         wide = pltpu.VMEM((num, dim), F32)
         head = pltpu.VMEM((num, hd), F32)
-        arrived = [pltpu.VMEM(hidden_in.shape, BF16), pltpu.VMEM(fresh, BF16), pltpu.VMEM(fresh, BF16), pltpu.VMEM(cache, BF16), pltpu.VMEM(cache, BF16)]
-        out, k_new, v_new, k_all, v_all = pl.pallas_call(
+        arrived = (pltpu.VMEM(hidden_in.shape, BF16), pltpu.VMEM(cache, BF16), pltpu.VMEM(cache, BF16))
+        held = pl.pallas_call(
             functools.partial(layer_kernel, n, steps, rows, heads, hd),
             name="layer",
-            out_shape=tuple(arrived),
+            out_shape=arrived,
             in_specs=[smem] + [hbm] * 15,
-            out_specs=(vmem,) * 5,
+            out_specs=(vmem,) * 3,
             scratch_shapes=[
                 pltpu.VMEM(freq.shape, F32), pltpu.VMEM(hidden_in.shape, BF16), pltpu.VMEM((dim,), BF16),
                 pltpu.VMEM((1, hd), BF16), pltpu.VMEM((1, hd), BF16), pltpu.VMEM((dim,), BF16),
@@ -465,8 +466,9 @@
                 blocks, blocks, chunk, chunk,
                 pltpu.VMEM((2, dim, TILE), BF16), pltpu.VMEM((2, dim, TILE), BF16), pltpu.VMEM((2, TILE, dim), BF16),
                 pltpu.VMEM((slots * n, hd), F32), pltpu.VMEM((num * n, hd), F32), pltpu.VMEM((num * n, hd), F32),
+                pltpu.VMEM((4, slots, hd), BF16),
                 dma((2,)), dma((2,)), dma((2,)), dma((2,)), dma((2,)), dma((2,)),
-                dma((n,)), dma((n,)), dma((n,)), dma((n,)), dma((2,)), dma((pairs,)), dma((pairs + PAIR + 1,)), dma((6,)), pltpu.SemaphoreType.REGULAR,
+                dma((n,)), dma((n,)), dma((n,)), dma((n,)), dma((2,)), dma((pairs,)), dma((pairs + PAIR + 1,)), dma((6,)), pltpu.SemaphoreType.REGULAR, dma((4,)),
             ],
             compiler_params=pltpu.CompilerParams(collective_id=0, has_side_effects=True, vmem_limit_bytes=VMEM_LIMIT),
         )(
@@ -476,15 +478,11 @@
         return pl.pallas_call(
             store_kernel,
             name="store",
-            out_shape=(
-                jax.ShapeDtypeStruct(hidden_in.shape, BF16), jax.ShapeDtypeStruct(cache, BF16), jax.ShapeDtypeStruct(cache, BF16),
-                pltpu.VMEM(cache, BF16), pltpu.VMEM(cache, BF16),
-            ),
-            in_specs=[smem] + [vmem] * 5,
-            out_specs=(hbm,) * 3 + (vmem,) * 2,
-            input_output_aliases={2: 3, 3: 4},
+            out_shape=tuple(jax.ShapeDtypeStruct(a.shape, BF16) for a in (hidden_in, held[1], held[2])),
+            in_specs=[vmem] * 3,
+            out_specs=(hbm,) * 3,
             scratch_shapes=[dma, dma((2, rows))],
             compiler_params=pltpu.CompilerParams(vmem_limit_bytes=2**20),
-        )(start_pos, out, k_all, v_all, k_new, v_new)[:3]
+        )(*held)
 
     return jax.shard_map(local_run, mesh=mesh, in_specs=(P("dp"), row_spec, cache_in, cache_in) + (P(),) * 11, out_specs=(row_spec, cache_out, cache_out), check_vma=False)

time: 197 us -> 197 us (level)
  no operation moved by 1% of the time
where the time goes in v6:
time: 197 us
  Pallas kernels  196 us (99%)
    pallas_call x1, Pallas kernels, local_run(): pl.pallas_call(functools.partial(layer_kernel, n, steps, rows, heads, hd)...  190 us
    pallas_call x1, Pallas kernels, local_run(): pl.pallas_call(store_kernel, name='store', out_shape=tuple((jax.ShapeDtyp...  6.15 us

profile of v6, /device:TPU:81, one launch (start us, length us, event | category | flops | bytes accessed | tf_op | source)
XLA Modules:
  0.0 196.6 jit_solution(12459600412138363477)
XLA Ops:
  0.6 189.8 %layer.1 = (bf16[4,16,2048]{2,1,0:T(8,128)(2,1)S(1)}, bf16[16,256,8,128]{3,2,1,0:T(8,128)(2,1)S(1)}, bf16[16,256,8,128]{3,2,1,0:T(8,128)(2,1)S(1)}) custom-call(s32[128]{0:T(128)} %pos_ref.1, f32[1,128]{1,0:T(1,128)} %constant.2.clone.freq_hbm, bf16[4,16,2048]{2,1,0:T(8,128)(2,1)} %hid_hbm.1, bf16[128,256,128]{2,1,0:T(8,128)(2,1)} %bitcast.4, ...), custom_call_target="tpu_custom_call" | custom-call | tf_op jit(solution)/shard_map/layer/pallas_call | solution.py:454
  190.4 6.2 %store.1 = (bf16[4,16,2048]{2,1,0:T(8,128)(2,1)}, bf16[16,256,8,128]{3,2,1,0:T(8,128)(2,1)}, bf16[16,256,8,128]{3,2,1,0:T(8,128)(2,1)}) custom-call(bf16[4,16,2048]{2,1,0:T(8,128)(2,1)S(1)} %get-tuple-element.6.hid_ref, bf16[16,256,8,128]{3,2,1,0:T(8,128)(2,1)S(1)} %get-tuple-element.7.ka_ref, bf16[16,256,8,128]{3,2,1,0:T(8,128)(2,1)S(1)} %get-tuple-element.8.va_ref), custom_call_target="tpu_custom_call" | custom-call | tf_op jit(solution)/shard_map/store/pallas_call | solution.py:478

commit v7 on v6

--- a/solution.py
+++ b/solution.py
@@ -17,7 +17,8 @@
 PAIR = 2
 AWAY = 2
 VMEM_LIMIT = 44 * 2**20
-AHEAD = 4
+UNIT = 4
+AHEAD = 2
 
 
 def rms(values, gain):
@@ -38,6 +39,8 @@
     q_per = heads // n
     pairs = rows // PAIR
     home = pairs - AWAY
+    rounds = rows // UNIT
+    per_unit = UNIT // PAIR
     slots = k_hbm.shape[1]
     dim = hid_ref.shape[2]
     tall = PAIR * steps * q_per
@@ -93,25 +96,25 @@
 
     mixed_order = [(1, False), (chips - 1, False)] + far[:1] + [(1, True), (chips - 1, True)] + far[1:] + [(0, True)]
     far_first = far + [(1, False), (chips - 1, False), (1, True), (chips - 1, True), (0, True)]
-    last = [(0, pairs - 1, rows - PAIR, PAIR, 0, slots)]
-    last += [(1, pairs - 1 + e, rows - PAIR + e, 1, 0, slots) for e in range(PAIR - 1)]
+    last = [(0, rounds - 1, rows - UNIT, UNIT, 0, slots), (1, rounds - 1, rows - UNIT, UNIT - 2, 0, slots)]
+    last.append((1, rounds, rows - 2, 1, 0, slots))
     for i, (lo, size) in enumerate(((0, slots // 2), (slots // 2, slots // 4), (slots * 3 // 4, slots // 4))):
-        last.append((1, pairs - 2 + PAIR + i, rows - 1, 1, lo, size))
+        last.append((1, rounds + 1 + i, rows - 1, 1, lo, size))
 
     def bulk(r):
-        send(0, r, r * PAIR, PAIR, 0, slots, mixed_order)
-        send(1, r, r * PAIR, PAIR, 0, slots, mixed_order)
+        send(0, r, r * UNIT, UNIT, 0, slots, mixed_order)
+        send(1, r, r * UNIT, UNIT, 0, slots, mixed_order)
 
     def bulk_last():
         for which, sem, first, count, lo, size in last:
             send(which, sem, first, count, lo, size, far_first)
 
     def bulk_next(r):
-        @pl.when(r < pairs - 1)
+        @pl.when(r < rounds - 1)
         def _():
             bulk(r)
 
-        @pl.when(r == pairs - 1)
+        @pl.when(r == rounds - 1)
         def _():
             bulk_last()
 
@@ -125,12 +128,11 @@
             src_ref=stage_s.at[i], dst_ref=rk.at[me, 0], send_sem=bulk_s.at[0], recv_sem=krs.at[0],
             device_id={"x": away(*to)}, device_id_type=MESH,
         ).start()
-    send(0, 0, 1, PAIR - 1, 0, slots, near[1:])
-    send(0, 0, 0, PAIR, 0, slots, near[:1])
+    send(0, 0, 1, UNIT - 1, 0, slots, near[1:])
+    send(0, 0, 0, UNIT, 0, slots, near[:1])
     pl.semaphore_wait(ready, 1)
-    send(0, 0, 0, PAIR, 0, slots, far)
-    send(1, 0, 0, PAIR, 0, slots, mixed_order)
-    bulk(1)
+    send(0, 0, 0, UNIT, 0, slots, far)
+    send(1, 0, 0, UNIT, 0, slots, mixed_order)
 
     own = [
         pltpu.make_async_copy(k_hbm.at[pl.ds(me * rows, rows)], rk.at[me], own_sem.at[0]),
@@ -243,7 +245,7 @@
     msg_r[me] = msg_s[me, home:pairs]
     for o in range(1, n):
         msg_copy(peer(o)).start()
-    for r in range(2, AHEAD):
+    for r in range(1, AHEAD):
         bulk(r)
 
     scale = hd ** -0.5
@@ -329,19 +331,21 @@
                 mixed = jnp.where(slot == pos_ref[me * rows + first + e] + s, fresh[None], mixed)
             dst[first + e, lo : lo + size] = mixed.astype(BF16)
 
-    @pl.loop(0, home)
+    @pl.loop(0, home // per_unit)
     def _(r):
-        bulk_wait(0, r, PAIR, slots)
-        bulk_wait(1, r, PAIR, slots)
+        bulk_wait(0, r, UNIT, slots)
+        bulk_wait(1, r, UNIT, slots)
         bulk_next(r + AHEAD)
-        place(0, r * PAIR, PAIR)
-        place(1, r * PAIR, PAIR)
+        place(0, r * UNIT, UNIT)
+        place(1, r * UNIT, UNIT)
 
         @pl.loop(0, n)
         def _(h):
-            o_r[h, r] = attend(
-                msg_s[h, r], lambda e: rk[h, r * PAIR + e], lambda e: rv[h, r * PAIR + e], me * rows + r * PAIR
-            )
+            for i in range(per_unit):
+                b = r * UNIT + i * PAIR
+                o_r[h, r * per_unit + i] = attend(
+                    msg_s[h, r * per_unit + i], lambda e: rk[h, b + e], lambda e: rv[h, b + e], me * rows + b
+                )
 
     for o in range(1, n):
         o_arrival(peer(o)).wait_recv()
@@ -397,12 +401,6 @@
     for o in range(1, n):
         msg_copy(peer(o)).wait_send()
         o_copy(peer(o)).wait_send()
-
-    @pl.loop(home, pairs - 1)
-    def _(r):
-        for which in range(2):
-            bulk_wait(which, r, PAIR, slots)
-            place(which, r * PAIR, PAIR)
 
     for which, sem, first, count, lo, size in last:
         bulk_wait(which, sem, count, size)
@@ -468,7 +466,7 @@
                 pltpu.VMEM((slots * n, hd), F32), pltpu.VMEM((num * n, hd), F32), pltpu.VMEM((num * n, hd), F32),
                 pltpu.VMEM((4, slots, hd), BF16),
                 dma((2,)), dma((2,)), dma((2,)), dma((2,)), dma((2,)), dma((2,)),
-                dma((n,)), dma((n,)), dma((n,)), dma((n,)), dma((2,)), dma((pairs,)), dma((pairs + PAIR + 1,)), dma((6,)), pltpu.SemaphoreType.REGULAR, dma((4,)),
+                dma((n,)), dma((n,)), dma((n,)), dma((n,)), dma((2,)), dma((rows // UNIT,)), dma((rows // UNIT + 4,)), dma((6,)), pltpu.SemaphoreType.REGULAR, dma((4,)),
             ],
             compiler_params=pltpu.CompilerParams(collective_id=0, has_side_effects=True, vmem_limit_bytes=VMEM_LIMIT),
         )(

time: 197 us -> 208 us (1.056)
  the two profiles are of different devices: /device:TPU:81 before, /device:TPU:87 now
where the time goes in v7:
time: 208 us
  Pallas kernels  207 us (100%)
    pallas_call x1, Pallas kernels, local_run(): pl.pallas_call(functools.partial(layer_kernel, n, steps, rows, heads, hd)...  201 us
    pallas_call x1, Pallas kernels, local_run(): pl.pallas_call(store_kernel, name='store', out_shape=tuple((jax.ShapeDtyp...  6.15 us

profile of v7, /device:TPU:87, one launch (start us, length us, event | category | flops | bytes accessed | tf_op | source)
XLA Modules:
  0.0 208.0 jit_solution(16374171919233264883)
XLA Ops:
  0.6 201.2 %layer.1 = (bf16[4,16,2048]{2,1,0:T(8,128)(2,1)S(1)}, bf16[16,256,8,128]{3,2,1,0:T(8,128)(2,1)S(1)}, bf16[16,256,8,128]{3,2,1,0:T(8,128)(2,1)S(1)}) custom-call(s32[128]{0:T(128)} %pos_ref.1, f32[1,128]{1,0:T(1,128)} %constant.2.clone.freq_hbm, bf16[4,16,2048]{2,1,0:T(8,128)(2,1)} %hid_hbm.1, bf16[128,256,128]{2,1,0:T(8,128)(2,1)} %bitcast.4, ...), custom_call_target="tpu_custom_call" | custom-call | tf_op jit(solution)/shard_map/layer/pallas_call | solution.py:452
  201.8 6.2 %store.1 = (bf16[4,16,2048]{2,1,0:T(8,128)(2,1)}, bf16[16,256,8,128]{3,2,1,0:T(8,128)(2,1)}, bf16[16,256,8,128]{3,2,1,0:T(8,128)(2,1)}) custom-call(bf16[4,16,2048]{2,1,0:T(8,128)(2,1)S(1)} %get-tuple-element.6.hid_ref, bf16[16,256,8,128]{3,2,1,0:T(8,128)(2,1)S(1)} %get-tuple-element.7.ka_ref, bf16[16,256,8,128]{3,2,1,0:T(8,128)(2,1)S(1)} %get-tuple-element.8.va_ref), custom_call_target="tpu_custom_call" | custom-call | tf_op jit(solution)/shard_map/store/pallas_call | solution.py:476

commit v8 on v6

--- a/solution.py
+++ b/solution.py
@@ -30,8 +30,8 @@
     pos_ref, freq_hbm, hid_hbm, k_hbm, v_hbm, an_hbm, wq_hbm, wk_hbm, wv_hbm, qn_hbm, kn_hbm, wo_hbm, mn_hbm,
     wg_hbm, wu_hbm, wd_hbm,
     out_ref, ka_ref, va_ref,
-    freq_ref, hid_ref, an_ref, qn_ref, kn_ref, mn_ref, hid_s, act_s, x1_s, acc_s, tmp_s, cs_s, sn_s, msg_s, msg_r, o_s, o_r, rk, rv, kbuf, vbuf, wbuf, ubuf, dbuf, mix_s, kmix_s, vmix_s, stage_s,
-    wsem, usem, dsem, ksem, vsem, own_sem, msg_ss, msg_rs, o_ss, o_rs, bulk_s, krs, vrs, in_sem, ready, stage_sem,
+    freq_ref, hid_ref, an_ref, qn_ref, kn_ref, mn_ref, hid_s, act_s, x1_s, acc_s, tmp_s, cs_s, sn_s, msg_s, msg_r, o_s, o_r, rk, rv, kbuf, vbuf, wbuf, ubuf, dbuf, mix_s, kmix_s, vmix_s,
+    wsem, usem, dsem, ksem, vsem, own_sem, msg_ss, msg_rs, o_ss, o_rs, bulk_s, krs, vrs, in_sem, ready,
 ):
     me = lax.axis_index("x")
     num = steps * rows
@@ -54,7 +54,6 @@
         return lax.rem(chip + hops, chips) * 2 + (1 - core if cross else core)
 
     near = [(0, True)] + [(hops, cross) for hops in (1, chips - 1) for cross in (False, True)]
-    far = [(hops, cross) for hops in range(2, chips - 1) for cross in (False, True)]
     for to in near:
         pl.semaphore_signal(barrier, inc=1, device_id={"x": away(*to)}, device_id_type=MESH)
 
@@ -73,17 +72,12 @@
     def load(src, dst, sem, slot):
         return pltpu.make_async_copy(src, dst.at[slot], sem.at[slot])
 
-    staged = [
-        pltpu.make_async_copy(k_hbm.at[away(*to) * rows], stage_s.at[i], stage_sem.at[i]) for i, to in enumerate(near[1:])
-    ]
-    for c in staged:
-        c.start()
     load(cols(wq_hbm, 0), wbuf, wsem, 0).start()
     pl.semaphore_wait(barrier, len(near))
     pl.semaphore_signal(ready, inc=1, device_id={"x": away(chips - 1, False)}, device_id_type=MESH)
 
-    def send(which, sem, first, count, lo, size, order):
-        for hops, cross in order:
+    def send(which, sem, first, count, lo, size, targets):
+        for hops, cross in targets:
             to = away(hops, cross)
             pltpu.make_async_remote_copy(
                 src_ref=(k_hbm, v_hbm)[which].at[pl.ds(to * rows + first, count), pl.ds(lo, size)],
@@ -91,20 +85,22 @@
                 send_sem=bulk_s.at[which], recv_sem=(krs, vrs)[which].at[sem], device_id={"x": to}, device_id_type=MESH,
             ).start()
 
-    mixed_order = [(1, False), (chips - 1, False)] + far[:1] + [(1, True), (chips - 1, True)] + far[1:] + [(0, True)]
-    far_first = far + [(1, False), (chips - 1, False), (1, True), (chips - 1, True), (0, True)]
+    turn = core * (chips - 2)
+    one_way, other_way = 1 + turn, chips - 1 - turn
+    order = [(hops, cross) for cross in (False, True) for hops in [one_way, *range(2, chips - 1), other_way]] + [(0, True)]
+
     last = [(0, pairs - 1, rows - PAIR, PAIR, 0, slots)]
     last += [(1, pairs - 1 + e, rows - PAIR + e, 1, 0, slots) for e in range(PAIR - 1)]
     for i, (lo, size) in enumerate(((0, slots // 2), (slots // 2, slots // 4), (slots * 3 // 4, slots // 4))):
         last.append((1, pairs - 2 + PAIR + i, rows - 1, 1, lo, size))
 
     def bulk(r):
-        send(0, r, r * PAIR, PAIR, 0, slots, mixed_order)
-        send(1, r, r * PAIR, PAIR, 0, slots, mixed_order)
+        send(0, r, r * PAIR, PAIR, 0, slots, order)
+        send(1, r, r * PAIR, PAIR, 0, slots, order)
 
     def bulk_last():
         for which, sem, first, count, lo, size in last:
-            send(which, sem, first, count, lo, size, far_first)
+            send(which, sem, first, count, lo, size, order)
 
     def bulk_next(r):
         @pl.when(r < pairs - 1)
@@ -119,17 +115,10 @@
         whole = (rk, rv)[which].at[pl.ds(0, n - 1), pl.ds(0, count), pl.ds(0, size)]
         pltpu.make_async_copy(whole, whole, (krs, vrs)[which].at[sem]).wait()
 
-    for i, to in enumerate(near[1:]):
-        staged[i].wait()
-        pltpu.make_async_remote_copy(
-            src_ref=stage_s.at[i], dst_ref=rk.at[me, 0], send_sem=bulk_s.at[0], recv_sem=krs.at[0],
-            device_id={"x": away(*to)}, device_id_type=MESH,
-        ).start()
-    send(0, 0, 1, PAIR - 1, 0, slots, near[1:])
-    send(0, 0, 0, PAIR, 0, slots, near[:1])
+    send(0, 0, 0, PAIR, 0, slots, order[:1])
     pl.semaphore_wait(ready, 1)
-    send(0, 0, 0, PAIR, 0, slots, far)
-    send(1, 0, 0, PAIR, 0, slots, mixed_order)
+    send(0, 0, 0, PAIR, 0, slots, order[1:])
+    send(1, 0, 0, PAIR, 0, slots, order)
     bulk(1)
 
     own = [
@@ -466,9 +455,8 @@
                 blocks, blocks, chunk, chunk,
                 pltpu.VMEM((2, dim, TILE), BF16), pltpu.VMEM((2, dim, TILE), BF16), pltpu.VMEM((2, TILE, dim), BF16),
                 pltpu.VMEM((slots * n, hd), F32), pltpu.VMEM((num * n, hd), F32), pltpu.VMEM((num * n, hd), F32),
-                pltpu.VMEM((4, slots, hd), BF16),
                 dma((2,)), dma((2,)), dma((2,)), dma((2,)), dma((2,)), dma((2,)),
-                dma((n,)), dma((n,)), dma((n,)), dma((n,)), dma((2,)), dma((pairs,)), dma((pairs + PAIR + 1,)), dma((6,)), pltpu.SemaphoreType.REGULAR, dma((4,)),
+                dma((n,)), dma((n,)), dma((n,)), dma((n,)), dma((2,)), dma((pairs,)), dma((pairs + PAIR + 1,)), dma((6,)), pltpu.SemaphoreType.REGULAR,
             ],
             compiler_params=pltpu.CompilerParams(collective_id=0, has_side_effects=True, vmem_limit_bytes=VMEM_LIMIT),
         )(

time: 197 us -> 197 us (level)
  no operation moved by 1% of the time
where the time goes in v8:
time: 197 us
  Pallas kernels  196 us (99%)
    pallas_call x1, Pallas kernels, local_run(): pl.pallas_call(functools.partial(layer_kernel, n, steps, rows, heads, hd)...  190 us
    pallas_call x1, Pallas kernels, local_run(): pl.pallas_call(store_kernel, name='store', out_shape=tuple((jax.ShapeDtyp...  6.15 us

profile of v8, /device:TPU:81, one launch (start us, length us, event | category | flops | bytes accessed | tf_op | source)
XLA Modules:
  0.0 197.0 jit_solution(2200765265487136226)
XLA Ops:
  0.6 190.2 %layer.1 = (bf16[4,16,2048]{2,1,0:T(8,128)(2,1)S(1)}, bf16[16,256,8,128]{3,2,1,0:T(8,128)(2,1)S(1)}, bf16[16,256,8,128]{3,2,1,0:T(8,128)(2,1)S(1)}) custom-call(s32[128]{0:T(128)} %pos_ref.1, f32[1,128]{1,0:T(1,128)} %constant.2.clone.freq_hbm, bf16[4,16,2048]{2,1,0:T(8,128)(2,1)} %hid_hbm.1, bf16[128,256,128]{2,1,0:T(8,128)(2,1)} %bitcast.4, ...), custom_call_target="tpu_custom_call" | custom-call | tf_op jit(solution)/shard_map/layer/pallas_call | solution.py:443
  190.8 6.2 %store.1 = (bf16[4,16,2048]{2,1,0:T(8,128)(2,1)}, bf16[16,256,8,128]{3,2,1,0:T(8,128)(2,1)}, bf16[16,256,8,128]{3,2,1,0:T(8,128)(2,1)}) custom-call(bf16[4,16,2048]{2,1,0:T(8,128)(2,1)S(1)} %get-tuple-element.6.hid_ref, bf16[16,256,8,128]{3,2,1,0:T(8,128)(2,1)S(1)} %get-tuple-element.7.ka_ref, bf16[16,256,8,128]{3,2,1,0:T(8,128)(2,1)S(1)} %get-tuple-element.8.va_ref), custom_call_target="tpu_custom_call" | custom-call | tf_op jit(solution)/shard_map/store/pallas_call | solution.py:466

commit v9 on v8

--- a/solution.py
+++ b/solution.py
@@ -27,10 +27,10 @@
 
 def layer_kernel(
     n, steps, rows, heads, hd,
-    pos_ref, freq_hbm, hid_hbm, k_hbm, v_hbm, an_hbm, wq_hbm, wk_hbm, wv_hbm, qn_hbm, kn_hbm, wo_hbm, mn_hbm,
+    pos_hbm, freq_hbm, hid_hbm, k_hbm, v_hbm, an_hbm, wq_hbm, wk_hbm, wv_hbm, qn_hbm, kn_hbm, wo_hbm, mn_hbm,
     wg_hbm, wu_hbm, wd_hbm,
     out_ref, ka_ref, va_ref,
-    freq_ref, hid_ref, an_ref, qn_ref, kn_ref, mn_ref, hid_s, act_s, x1_s, acc_s, tmp_s, cs_s, sn_s, msg_s, msg_r, o_s, o_r, rk, rv, kbuf, vbuf, wbuf, ubuf, dbuf, mix_s, kmix_s, vmix_s,
+    pos_ref, freq_ref, hid_ref, an_ref, qn_ref, kn_ref, mn_ref, hid_s, act_s, x1_s, acc_s, tmp_s, cs_s, sn_s, msg_s, msg_r, o_s, o_r, rk, rv, kbuf, vbuf, wbuf, ubuf, dbuf, mix_s, kmix_s, vmix_s,
     wsem, usem, dsem, ksem, vsem, own_sem, msg_ss, msg_rs, o_ss, o_rs, bulk_s, krs, vrs, in_sem, ready,
 ):
     me = lax.axis_index("x")
@@ -60,7 +60,7 @@
     small = [
         pltpu.make_async_copy(src, dst, in_sem.at[i])
         for i, (src, dst) in enumerate((
-            (hid_hbm, hid_ref), (an_hbm, an_ref), (freq_hbm, freq_ref), (qn_hbm, qn_ref), (kn_hbm, kn_ref), (mn_hbm, mn_ref),
+            (hid_hbm, hid_ref), (an_hbm, an_ref), (freq_hbm, freq_ref), (qn_hbm, qn_ref), (kn_hbm, kn_ref), (mn_hbm, mn_ref), (pos_hbm, pos_ref),
         ))
     ]
     for c in small:
@@ -431,7 +431,6 @@
         freq = jnp.asarray(np.concatenate([inv_freq, inv_freq])[None, :], F32)
         vmem = pl.BlockSpec(memory_space=pltpu.VMEM)
         hbm = pl.BlockSpec(memory_space=pltpu.HBM)
-        smem = pl.BlockSpec(memory_space=pltpu.SMEM)
         tall, new = PAIR * steps * (heads // n), PAIR * steps
         dma = pltpu.SemaphoreType.DMA
         cache = (rows, slots, n, hd)
@@ -444,10 +443,10 @@
             functools.partial(layer_kernel, n, steps, rows, heads, hd),
             name="layer",
             out_shape=arrived,
-            in_specs=[smem] + [hbm] * 15,
+            in_specs=[hbm] * 16,
             out_specs=(vmem,) * 3,
             scratch_shapes=[
-                pltpu.VMEM(freq.shape, F32), pltpu.VMEM(hidden_in.shape, BF16), pltpu.VMEM((dim,), BF16),
+                pltpu.SMEM(start_pos.shape, jnp.int32), pltpu.VMEM(freq.shape, F32), pltpu.VMEM(hidden_in.shape, BF16), pltpu.VMEM((dim,), BF16),
                 pltpu.VMEM((1, hd), BF16), pltpu.VMEM((1, hd), BF16), pltpu.VMEM((dim,), BF16),
                 wide, pltpu.VMEM((num, dim), BF16), wide, wide, head, head, head,
                 pltpu.VMEM((n, pairs, tall + 2 * new, hd), BF16), pltpu.VMEM((n, AWAY, tall + 2 * new, hd), BF16),
@@ -456,7 +455,7 @@
                 pltpu.VMEM((2, dim, TILE), BF16), pltpu.VMEM((2, dim, TILE), BF16), pltpu.VMEM((2, TILE, dim), BF16),
                 pltpu.VMEM((slots * n, hd), F32), pltpu.VMEM((num * n, hd), F32), pltpu.VMEM((num * n, hd), F32),
                 dma((2,)), dma((2,)), dma((2,)), dma((2,)), dma((2,)), dma((2,)),
-                dma((n,)), dma((n,)), dma((n,)), dma((n,)), dma((2,)), dma((pairs,)), dma((pairs + PAIR + 1,)), dma((6,)), pltpu.SemaphoreType.REGULAR,
+                dma((n,)), dma((n,)), dma((n,)), dma((n,)), dma((2,)), dma((pairs,)), dma((pairs + PAIR + 1,)), dma((7,)), pltpu.SemaphoreType.REGULAR,
             ],
             compiler_params=pltpu.CompilerParams(collective_id=0, has_side_effects=True, vmem_limit_bytes=VMEM_LIMIT),
         )(

time: 197 us -> 197 us (level)
  no operation moved by 1% of the time
where the time goes in v9:
time: 197 us; the launch traced here: 196 us
  Pallas kernels  196 us (99%)
    pallas_call x1, Pallas kernels, local_run(): pl.pallas_call(functools.partial(layer_kernel, n, steps, rows, heads, hd)...  190 us
    pallas_call x1, Pallas kernels, local_run(): pl.pallas_call(store_kernel, name='store', out_shape=tuple((jax.ShapeDtyp...  6.15 us

profile of v9, /device:TPU:81, one launch (start us, length us, event | category | flops | bytes accessed | tf_op | source)
XLA Modules:
  0.0 196.3 jit_solution(4522187543470552430)
XLA Ops:
  0.6 189.5 %layer.1 = (bf16[4,16,2048]{2,1,0:T(8,128)(2,1)S(1)}, bf16[16,256,8,128]{3,2,1,0:T(8,128)(2,1)S(1)}, bf16[16,256,8,128]{3,2,1,0:T(8,128)(2,1)S(1)}) custom-call(s32[128]{0:T(128)} %pos_hbm.1, f32[1,128]{1,0:T(1,128)} %constant.2.clone.freq_hbm, bf16[4,16,2048]{2,1,0:T(8,128)(2,1)} %hid_hbm.1, bf16[128,256,128]{2,1,0:T(8,128)(2,1)} %bitcast.4, ...), custom_call_target="tpu_custom_call" | custom-call | tf_op jit(solution)/shard_map/layer/pallas_call | solution.py:442
  190.2 6.2 %store.1 = (bf16[4,16,2048]{2,1,0:T(8,128)(2,1)}, bf16[16,256,8,128]{3,2,1,0:T(8,128)(2,1)}, bf16[16,256,8,128]{3,2,1,0:T(8,128)(2,1)}) custom-call(bf16[4,16,2048]{2,1,0:T(8,128)(2,1)S(1)} %get-tuple-element.6.hid_ref, bf16[16,256,8,128]{3,2,1,0:T(8,128)(2,1)S(1)} %get-tuple-element.7.ka_ref, bf16[16,256,8,128]{3,2,1,0:T(8,128)(2,1)S(1)} %get-tuple-element.8.va_ref), custom_call_target="tpu_custom_call" | custom-call | tf_op jit(solution)/shard_map/store/pallas_call | solution.py:465

commit v10 on v9

--- a/solution.py
+++ b/solution.py
@@ -53,7 +53,7 @@
     def away(hops, cross):
         return lax.rem(chip + hops, chips) * 2 + (1 - core if cross else core)
 
-    near = [(0, True)] + [(hops, cross) for hops in (1, chips - 1) for cross in (False, True)]
+    near = [(0, True), (1, False), (1, True), (chips - 1, False), (chips - 1, True)]
     for to in near:
         pl.semaphore_signal(barrier, inc=1, device_id={"x": away(*to)}, device_id_type=MESH)
 
@@ -85,9 +85,9 @@
                 send_sem=bulk_s.at[which], recv_sem=(krs, vrs)[which].at[sem], device_id={"x": to}, device_id_type=MESH,
             ).start()
 
-    turn = core * (chips - 2)
-    one_way, other_way = 1 + turn, chips - 1 - turn
-    order = [(hops, cross) for cross in (False, True) for hops in [one_way, *range(2, chips - 1), other_way]] + [(0, True)]
+    far = [(hops, cross) for hops in range(2, chips - 1) for cross in (False, True)]
+    order = near[1::2] + far[:1] + near[2::2] + far[1:] + near[:1]
+    far_first = far + near[1::2] + near[2::2] + near[:1]
 
     last = [(0, pairs - 1, rows - PAIR, PAIR, 0, slots)]
     last += [(1, pairs - 1 + e, rows - PAIR + e, 1, 0, slots) for e in range(PAIR - 1)]
@@ -100,7 +100,7 @@
 
     def bulk_last():
         for which, sem, first, count, lo, size in last:
-            send(which, sem, first, count, lo, size, order)
+            send(which, sem, first, count, lo, size, far_first)
 
     def bulk_next(r):
         @pl.when(r < pairs - 1)
@@ -115,9 +115,9 @@
         whole = (rk, rv)[which].at[pl.ds(0, n - 1), pl.ds(0, count), pl.ds(0, size)]
         pltpu.make_async_copy(whole, whole, (krs, vrs)[which].at[sem]).wait()
 
-    send(0, 0, 0, PAIR, 0, slots, order[:1])
+    send(0, 0, 0, PAIR, 0, slots, near[1:] + near[:1])
     pl.semaphore_wait(ready, 1)
-    send(0, 0, 0, PAIR, 0, slots, order[1:])
+    send(0, 0, 0, PAIR, 0, slots, far)
     send(1, 0, 0, PAIR, 0, slots, order)
     bulk(1)
 

time: 197 us -> 196 us (level)
  no operation moved by 1% of the time
where the time goes in v10:
time: 196 us
  Pallas kernels  195 us (99%)
    pallas_call x1, Pallas kernels, local_run(): pl.pallas_call(functools.partial(layer_kernel, n, steps, rows, heads, hd)...  189 us
    pallas_call x1, Pallas kernels, local_run(): pl.pallas_call(store_kernel, name='store', out_shape=tuple((jax.ShapeDtyp...  6.15 us

profile of v10, /device:TPU:81, one launch (start us, length us, event | category | flops | bytes accessed | tf_op | source)
XLA Modules:
  0.0 195.9 jit_solution(8323753076594705374)
XLA Ops:
  0.6 189.1 %layer.1 = (bf16[4,16,2048]{2,1,0:T(8,128)(2,1)S(1)}, bf16[16,256,8,128]{3,2,1,0:T(8,128)(2,1)S(1)}, bf16[16,256,8,128]{3,2,1,0:T(8,128)(2,1)S(1)}) custom-call(s32[128]{0:T(128)} %pos_hbm.1, f32[1,128]{1,0:T(1,128)} %constant.2.clone.freq_hbm, bf16[4,16,2048]{2,1,0:T(8,128)(2,1)} %hid_hbm.1, bf16[128,256,128]{2,1,0:T(8,128)(2,1)} %bitcast.4, ...), custom_call_target="tpu_custom_call" | custom-call | tf_op jit(solution)/shard_map/layer/pallas_call | solution.py:442
  189.7 6.2 %store.1 = (bf16[4,16,2048]{2,1,0:T(8,128)(2,1)}, bf16[16,256,8,128]{3,2,1,0:T(8,128)(2,1)}, bf16[16,256,8,128]{3,2,1,0:T(8,128)(2,1)}) custom-call(bf16[4,16,2048]{2,1,0:T(8,128)(2,1)S(1)} %get-tuple-element.6.hid_ref, bf16[16,256,8,128]{3,2,1,0:T(8,128)(2,1)S(1)} %get-tuple-element.7.ka_ref, bf16[16,256,8,128]{3,2,1,0:T(8,128)(2,1)S(1)} %get-tuple-element.8.va_ref), custom_call_target="tpu_custom_call" | custom-call | tf_op jit(solution)/shard_map/store/pallas_call | solution.py:465

commit v11 on v10

--- a/solution.py
+++ b/solution.py
@@ -95,8 +95,9 @@
         last.append((1, pairs - 2 + PAIR + i, rows - 1, 1, lo, size))
 
     def bulk(r):
-        send(0, r, r * PAIR, PAIR, 0, slots, order)
-        send(1, r, r * PAIR, PAIR, 0, slots, order)
+        for e in range(PAIR):
+            for which in range(2):
+                send(which, r, r * PAIR + e, 1, 0, slots, order)
 
     def bulk_last():
         for which, sem, first, count, lo, size in last:
@@ -115,10 +116,12 @@
         whole = (rk, rv)[which].at[pl.ds(0, n - 1), pl.ds(0, count), pl.ds(0, size)]
         pltpu.make_async_copy(whole, whole, (krs, vrs)[which].at[sem]).wait()
 
-    send(0, 0, 0, PAIR, 0, slots, near[1:] + near[:1])
+    send(0, 0, 0, 1, 0, slots, near[1:] + near[:1])
     pl.semaphore_wait(ready, 1)
-    send(0, 0, 0, PAIR, 0, slots, far)
-    send(1, 0, 0, PAIR, 0, slots, order)
+    send(0, 0, 0, 1, 0, slots, far)
+    send(1, 0, 0, 1, 0, slots, order)
+    for which in range(2):
+        send(which, 0, 1, PAIR - 1, 0, slots, order)
     bulk(1)
 
     own = [

time: 196 us -> 196 us (level)
  no operation moved by 1% of the time
where the time goes in v11:
time: 196 us
  Pallas kernels  195 us (99%)
    pallas_call x1, Pallas kernels, local_run(): pl.pallas_call(functools.partial(layer_kernel, n, steps, rows, heads, hd)...  189 us
    pallas_call x1, Pallas kernels, local_run(): pl.pallas_call(store_kernel, name='store', out_shape=tuple((jax.ShapeDtyp...  6.15 us

profile of v11, /device:TPU:81, one launch (start us, length us, event | category | flops | bytes accessed | tf_op | source)
XLA Modules:
  0.0 195.7 jit_solution(11693182929127081075)
XLA Ops:
  0.6 188.9 %layer.1 = (bf16[4,16,2048]{2,1,0:T(8,128)(2,1)S(1)}, bf16[16,256,8,128]{3,2,1,0:T(8,128)(2,1)S(1)}, bf16[16,256,8,128]{3,2,1,0:T(8,128)(2,1)S(1)}) custom-call(s32[128]{0:T(128)} %pos_hbm.1, f32[1,128]{1,0:T(1,128)} %constant.2.clone.freq_hbm, bf16[4,16,2048]{2,1,0:T(8,128)(2,1)} %hid_hbm.1, bf16[128,256,128]{2,1,0:T(8,128)(2,1)} %bitcast.4, ...), custom_call_target="tpu_custom_call" | custom-call | tf_op jit(solution)/shard_map/layer/pallas_call | solution.py:445
  189.6 6.2 %store.1 = (bf16[4,16,2048]{2,1,0:T(8,128)(2,1)}, bf16[16,256,8,128]{3,2,1,0:T(8,128)(2,1)}, bf16[16,256,8,128]{3,2,1,0:T(8,128)(2,1)}) custom-call(bf16[4,16,2048]{2,1,0:T(8,128)(2,1)S(1)} %get-tuple-element.6.hid_ref, bf16[16,256,8,128]{3,2,1,0:T(8,128)(2,1)S(1)} %get-tuple-element.7.ka_ref, bf16[16,256,8,128]{3,2,1,0:T(8,128)(2,1)S(1)} %get-tuple-element.8.va_ref), custom_call_target="tpu_custom_call" | custom-call | tf_op jit(solution)/shard_map/store/pallas_call | solution.py:468

commit v12 on v11

--- a/solution.py
+++ b/solution.py
@@ -91,7 +91,7 @@
 
     last = [(0, pairs - 1, rows - PAIR, PAIR, 0, slots)]
     last += [(1, pairs - 1 + e, rows - PAIR + e, 1, 0, slots) for e in range(PAIR - 1)]
-    for i, (lo, size) in enumerate(((0, slots // 2), (slots // 2, slots // 4), (slots * 3 // 4, slots // 4))):
+    for i, (lo, size) in enumerate(((0, slots // 2), (slots // 2, slots // 2))):
         last.append((1, pairs - 2 + PAIR + i, rows - 1, 1, lo, size))
 
     def bulk(r):
@@ -407,9 +407,12 @@
 
 def store_kernel(hid_ref, ka_ref, va_ref, out_hbm, ko_hbm, vo_hbm, hid_sem, sems):
     copies = []
-    for b in range(ka_ref.shape[0]):
-        copies.append(pltpu.make_async_copy(ka_ref.at[b], ko_hbm.at[b], sems.at[0, b]))
-        copies.append(pltpu.make_async_copy(va_ref.at[b], vo_hbm.at[b], sems.at[1, b]))
+    parts = sems.shape[1]
+    size = ka_ref.shape[0] // parts
+    for b in range(parts):
+        at = pl.ds(b * size, size)
+        copies.append(pltpu.make_async_copy(ka_ref.at[at], ko_hbm.at[at], sems.at[0, b]))
+        copies.append(pltpu.make_async_copy(va_ref.at[at], vo_hbm.at[at], sems.at[1, b]))
     copies.append(pltpu.make_async_copy(hid_ref, out_hbm, hid_sem))
     for c in copies:
         c.start()
@@ -458,7 +461,7 @@
                 pltpu.VMEM((2, dim, TILE), BF16), pltpu.VMEM((2, dim, TILE), BF16), pltpu.VMEM((2, TILE, dim), BF16),
                 pltpu.VMEM((slots * n, hd), F32), pltpu.VMEM((num * n, hd), F32), pltpu.VMEM((num * n, hd), F32),
                 dma((2,)), dma((2,)), dma((2,)), dma((2,)), dma((2,)), dma((2,)),
-                dma((n,)), dma((n,)), dma((n,)), dma((n,)), dma((2,)), dma((pairs,)), dma((pairs + PAIR + 1,)), dma((7,)), pltpu.SemaphoreType.REGULAR,
+                dma((n,)), dma((n,)), dma((n,)), dma((n,)), dma((2,)), dma((pairs,)), dma((pairs + PAIR,)), dma((7,)), pltpu.SemaphoreType.REGULAR,
             ],
             compiler_params=pltpu.CompilerParams(collective_id=0, has_side_effects=True, vmem_limit_bytes=VMEM_LIMIT),
         )(
@@ -471,7 +474,7 @@
             out_shape=tuple(jax.ShapeDtypeStruct(a.shape, BF16) for a in (hidden_in, held[1], held[2])),
             in_specs=[vmem] * 3,
             out_specs=(hbm,) * 3,
-            scratch_shapes=[dma, dma((2, rows))],
+            scratch_shapes=[dma, dma((2, 4))],
             compiler_params=pltpu.CompilerParams(vmem_limit_bytes=2**20),
         )(*held)
 

time: 196 us -> 195 us (level)
  no operation moved by 1% of the time
where the time goes in v12:
time: 195 us
  Pallas kernels  195 us (100%)
    pallas_call x1, Pallas kernels, local_run(): pl.pallas_call(functools.partial(layer_kernel, n, steps, rows, heads, hd)...  189 us
    pallas_call x1, Pallas kernels, local_run(): pl.pallas_call(store_kernel, name='store', out_shape=tuple((jax.ShapeDtyp...  5.95 us

profile of v12, /device:TPU:81, one launch (start us, length us, event | category | flops | bytes accessed | tf_op | source)
XLA Modules:
  0.0 195.2 jit_solution(2846847471642790841)
XLA Ops:
  0.6 188.6 %layer.1 = (bf16[4,16,2048]{2,1,0:T(8,128)(2,1)S(1)}, bf16[16,256,8,128]{3,2,1,0:T(8,128)(2,1)S(1)}, bf16[16,256,8,128]{3,2,1,0:T(8,128)(2,1)S(1)}) custom-call(s32[128]{0:T(128)} %pos_hbm.1, f32[1,128]{1,0:T(1,128)} %constant.2.clone.freq_hbm, bf16[4,16,2048]{2,1,0:T(8,128)(2,1)} %hid_hbm.1, bf16[128,256,128]{2,1,0:T(8,128)(2,1)} %bitcast.4, ...), custom_call_target="tpu_custom_call" | custom-call | tf_op jit(solution)/shard_map/layer/pallas_call | solution.py:448
  189.2 5.9 %store.1 = (bf16[4,16,2048]{2,1,0:T(8,128)(2,1)}, bf16[16,256,8,128]{3,2,1,0:T(8,128)(2,1)}, bf16[16,256,8,128]{3,2,1,0:T(8,128)(2,1)}) custom-call(bf16[4,16,2048]{2,1,0:T(8,128)(2,1)S(1)} %get-tuple-element.6.hid_ref, bf16[16,256,8,128]{3,2,1,0:T(8,128)(2,1)S(1)} %get-tuple-element.7.ka_ref, bf16[16,256,8,128]{3,2,1,0:T(8,128)(2,1)S(1)} %get-tuple-element.8.va_ref), custom_call_target="tpu_custom_call" | custom-call | tf_op jit(solution)/shard_map/store/pallas_call | solution.py:471
